TPU v7x, 512 devices: a whole 4x8x8 slice. The times are simulated.
512 devices in a mesh: gy: 32 (over z, y_lo), gz: 16 (over x, y_hi, core).
Axes of the slice: x: 4, y: 8 (y_hi: 2, y_lo: 4; y = y_hi * 4 + y_lo), z: 8, core: 2. Of those that a mesh axis runs over, the one named last changes fastest.
Arguments:
- scalar: float32 [64, 768, 768], P('gz', 'gy'), may hold values from -6 to 6
- velocity: float32 [3, 64, 256, 256], P(None, None, 'gy', 'gz'), may hold values from -0.9 to 0.9
Outputs:
- remeshed: float32 [64, 768, 768], P('gz', 'gy')
All inputs are finite; a program needn't handle non-finite values.
Results may differ from a plain program's by a relative error of at most 0.0003.
Values sent between devices are 32-bit elements; how exact they have to be, the bound alone decides.
No kernel may reach another device: no remote copies, remote signals or barrier semaphores. Data moves between devices by JAX's collectives and lax.ppermute only.
A program may use at most 64 MiB of HBM per device.

v0:
```python
import jax
import jax.numpy as jnp
from jax import lax
from jax.sharding import PartitionSpec as P


def padded_2(value, sides, width):
    for axis, dim in sides:
        peers, length = (lax.axis_size(axis), value.shape[dim])
        up = [(i, (i + 1) % peers) for i in range(peers - 1)]
        down = [(j, i) for i, j in up]
        last = lax.slice_in_dim(value, length - width, length, axis=dim)
        initial = lax.slice_in_dim(value, 0, width, axis=dim)
        before = lax.ppermute(last, axis, up)
        after = lax.ppermute(initial, axis, down)
        value = jnp.concatenate([before, value, after], axis=dim)
    return value


def passed_along(block, axis, distance):
    devices = range(lax.axis_size(axis))
    route = [((i - distance) % len(devices), i) for i in devices]
    return lax.ppermute(block, axis, route)


def alternate(current, following, along):
    pieces = [current * (1.0 - phase / 3.0) + following * (phase / 3.0) for phase in range(3)]
    stacked = jnp.stack(pieces, axis=along + 1)
    new_shape = list(current.shape)
    new_shape[along] = new_shape[along] * 3
    return stacked.reshape(new_shape)


def polynomial(factors, value):
    result = jnp.zeros_like(value)
    for factor in reversed(factors):
        result = result * value + factor
    return result


def kernel_weight(offset):
    size = jnp.abs(offset)
    inner = polynomial([1.0, 0.0, -5.0 / 4.0, -35.0 / 12.0, 21.0 / 4.0, -25.0 / 12.0], size)
    middle = polynomial(
        [-4.0, 75.0 / 4.0, -245.0 / 8.0, 545.0 / 24.0, -63.0 / 8.0, 25.0 / 24.0], size
    )
    outer = polynomial(
        [18.0, -153.0 / 4.0, 255.0 / 8.0, -313.0 / 24.0, 21.0 / 8.0, -5.0 / 24.0], size
    )
    return jnp.where(
        size < 1.0, inner, jnp.where(size < 2.0, middle, jnp.where(size < 3.0, outer, 0.0))
    )


def displacement(speed, before, after):
    half_step = 0.5 * speed
    return jnp.where(
        half_step >= 0.0,
        (1.0 - half_step) * speed + half_step * after,
        (1.0 + half_step) * speed - half_step * before,
    )


def sweep_periodic(field, speed, along):
    moved = displacement(speed, jnp.roll(speed, 1, along), jnp.roll(speed, -1, along))
    result = jnp.zeros_like(field)
    for offset in range(-3, 4):
        result = result + jnp.roll(field * kernel_weight(offset - moved), offset, along)
    return result


def sweep_open(field, speed, padded):
    padded = padded_2(speed, (("gz", 0),), 1)
    moved = displacement(speed, padded[:-2], padded[2:])
    count = field.shape[0]
    total = jnp.zeros((count + 6,) + field.shape[1:], jnp.float32)
    for offset in range(-3, 4):
        total = total.at[3 + offset : 3 + offset + count].add(field * kernel_weight(offset - moved))
    ghosts = jnp.concatenate([total[:3], total[count + 3 :]], axis=0)
    received = padded_2(ghosts, (("gz", 0),), 3)
    result = total[3 : count + 3]
    result = result.at[:3].add(received[:3])
    result = result.at[count - 3 :].add(received[9:])
    return result


def local(scalar, velocity):
    coarse = lax.all_to_all(velocity, "gz", split_axis=1, concat_axis=3, tiled=True)
    rows_part = coarse[:1]
    next_row = passed_along(rows_part[:, :, :1, :], "gy", -1)
    y_fine = alternate(rows_part, jnp.concatenate([rows_part[:, :, 1:, :], next_row], axis=2), 2)
    fine_vel = alternate(y_fine, jnp.roll(y_fine, -1, 3), 3)
    field = sweep_periodic(scalar, fine_vel[0], 2)
    turned = jnp.swapaxes(field, 1, 2)
    padded_z = None
    sending = coarse[1:]
    field = lax.all_to_all(turned, "gy", split_axis=1, concat_axis=2, tiled=True)
    coarse_rows = jnp.swapaxes(sending, 2, 3)
    coarse_turned = lax.all_to_all(coarse_rows, "gy", split_axis=2, concat_axis=3, tiled=True)
    y_refined = alternate(coarse_turned, jnp.roll(coarse_turned, -1, 3), 3)
    next_col = passed_along(y_refined[:, :, :1, :], "gy", -1)
    pencil_vel = alternate(
        y_refined, jnp.concatenate([y_refined[:, :, 1:, :], next_col], axis=2), 2
    )
    speed_y = pencil_vel[0]
    speed_z = pencil_vel[1]
    field = sweep_periodic(field, speed_y, 2)
    return sweep_open(field, speed_z, padded_z)


def solution(mesh):
    in_specs = (P("gz", "gy", None), P(None, None, "gy", "gz"))
    out_specs = P("gz", "gy", None)
    return jax.shard_map(local, mesh=mesh, in_specs=in_specs, out_specs=out_specs, check_vma=False)
```

profile of v0, /device:TPU:1, one launch (start us, length us, event | category | flops | bytes accessed | tf_op | source)
XLA Modules:
  0.0 137.3 jit_solution(2114219624516840462)
XLA Ops:
  0.0 1.2 copy.400
  1.6 20.6 %all_to_all.54 = f32[16,1,1536]{2,1,0:T(1,128)S(1)} all-to-all(f32[16,1,1536]{2,1,0:T(1,128)S(1)} %reshape.847), channel_id=1, replica_groups=mesh['gy'=32,'gz'=16] {'gz'}, dimensions={0} | all-to-all | bytes 196608 | tf_op jit(solution)/shard_map/all_to_all | solution.py:88
  22.2 0.6 broadcast.909
  22.7 0.8 reduce.18
  24.3 11.1 %collective-permute-start = (f32[1,4,1,256]{3,2,1,0:T(1,128)S(1)}, f32[1,4,1,256]{3,2,1,0:T(1,128)S(1)}, u32[]{:S(2)}, u32[]{:S(2)}) collective-permute-start(f32[1,4,1,256]{3,2,1,0:T(1,128)S(1)} %slice.470), channel_id=1, source_target_pairs={{16,0},{32,16},{48,32},{64,48},{80,64},{96,80},{112,96},{128,112},... | collective-permute-start | bytes 12296 | tf_op jit(solution)/shard_map/ppermute | solution.py:23
  36.6 1.8 %reshape.851 = f32[32,1,512]{2,1,0:T(1,128)} reshape(f32[256,2,4,8]{3,2,1,0:T(4,128)S(1)} %bitcast.82) | data formatting | bytes 131072
  38.4 3.9 %all-to-all-start.2 = ((f32[32,1,512]{2,1,0:T(1,128)}), f32[32,1,512]{2,1,0:T(1,128)S(1)}, u32[]{:S(2)}, u32[]{:S(2)}) async-start(f32[32,1,512]{2,1,0:T(1,128)} %reshape.851), calls=%async_computation.2 | async-start | bytes 131072 | tf_op jit(solution)/shard_map/all_to_all | solution.py:99
  42.9 0.8 copy.409
  43.7 0.6 copy.410
  44.5 0.6 fusion.25
  45.1 2.0 %fusion.22 = (f32[4,24,768]{2,1,0:T(8,128)S(1)}, f32[4,24,768]{2,1,0:T(8,128)S(1)}, f32[4,24,768]{2,1,0:T(8,128)S(1)}, f32[4,24,768]{2,1,0:T(8,128)S(1)}, f32[4,24,768]{2,1,0:T(8,128)S(1)}) fusion(f32[4,24,768]{2,1,0:T(8,128)S(1)} %copy-done, f32[4,24,768]{2,1,0:T(8,128)S(1)} %get-tuple-element.121), kind=kLoop, calls=%fused_computation.47 | loop fusion | flops 15482880 | bytes 2064384 | tf_op jit(solution)/shard_map/mul | solution.py:68
  47.8 0.5 fusion.16
  48.4 0.7 copy.417
  49.1 2.8 %reshape.849 = f32[32,1,2304]{2,1,0:T(1,128)} reshape(f32[768,4,24]{2,1,0:T(4,128)S(1)} %bitcast.76) | data formatting | bytes 589824
  51.9 9.7 %all-to-all-start.1 = ((f32[32,1,2304]{2,1,0:T(1,128)}), f32[32,1,2304]{2,1,0:T(1,128)S(1)}, u32[]{:S(2)}, u32[]{:S(2)}) async-start(f32[32,1,2304]{2,1,0:T(1,128)} %reshape.849), calls=%async_computation.1 | async-start | bytes 589824 | tf_op jit(solution)/shard_map/all_to_all | solution.py:97
  61.6 0.8 reduce.19
  62.4 1.2 reshape.852
  63.6 0.6 copy.465
  64.3 0.5 all_to_all.50
  64.9 0.5 all_to_all.49
  65.5 0.7 pad_maximum_fusion.4
  66.2 2.6 %copy.426 = f32[2,4,8,256,3]{2,1,4,3,0:T(4,128)S(1)} copy(f32[2,4,8,256,3]{3,2,1,0,4:T(8,128)} %pad_maximum_fusion.4) | data formatting | bytes 393216 | tf_op jit(solution)/shard_map/stack | solution.py:28
  68.8 1.2 copy.428
  70.0 7.0 %collective-permute-start.1 = (f32[2,4,1,768]{3,1,2,0:T(4,128)S(1)}, f32[2,4,1,768]{3,1,2,0:T(4,128)S(1)}, u32[]{:S(2)}, u32[]{:S(2)}) collective-permute-start(f32[2,4,1,768]{3,1,2,0:T(4,128)S(1)} %copy.428), channel_id=1, source_target_pairs={{16,0},{32,16},{48,32},{64,48},{80,64},{96,80},{112,96},{128,112},... | collective-permute-start | bytes 73736 | tf_op jit(solution)/shard_map/ppermute | solution.py:23
  77.0 3.3 %slice_bitcast_fusion = f32[2,4,7,1,768]{2,1,4,0,3:T(4,128)} fusion(f32[2,4,8,768]{2,1,3,0:T(4,128)S(1)} %bitcast.71), kind=kLoop, calls=%fused_computation | loop fusion | bytes 344064 | tf_op jit(solution)/shard_map/concatenate | solution.py:103
  80.3 3.8 %copy.429 = f32[2,4,7,1,768]{4,2,3,1,0:T(8,128)} copy(f32[2,4,7,1,768]{2,1,4,0,3:T(4,128)} %slice_bitcast_fusion) | data formatting | bytes 344064 | tf_op jit(solution)/shard_map/concatenate | solution.py:103
  84.1 2.0 %copy.431 = f32[2,4,8,1,768]{4,2,3,1,0:T(8,128)} copy(f32[2,4,8,1,768]{2,1,4,0,3:T(4,128)S(1)} %bitcast.72) | data formatting | bytes 393216 | tf_op jit(solution)/shard_map/reshape | solution.py:31
  86.1 1.1 multiply_add_fusion.24
  87.6 3.9 %collective-permute-start.2 = (f32[1,24,768]{2,0,1:T(1,128)S(1)}, f32[1,24,768]{2,0,1:T(1,128)S(1)}, u32[]{:S(2)}, u32[]{:S(2)}) collective-permute-start(f32[1,24,768]{2,0,1:T(1,128)S(1)} %bitcast.98), channel_id=1, source_target_pairs={{1,0},{2,1},{3,2},{4,3},{5,4},{6,5},{7,6},{8,7},{9,8},{10,9},{11,1... | collective-permute-start | bytes 221192 | tf_op jit(solution)/shard_map/ppermute | solution.py:15
  91.6 5.6 %collective-permute-start.3 = (f32[1,24,768]{2,0,1:T(1,128)S(1)}, f32[1,24,768]{2,0,1:T(1,128)S(1)}, u32[]{:S(2)}, u32[]{:S(2)}) collective-permute-start(f32[1,24,768]{2,0,1:T(1,128)S(1)} %bitcast.99), channel_id=1, source_target_pairs={{0,1},{1,2},{2,3},{3,4},{4,5},{5,6},{6,7},{7,8},{8,9},{9,10},{10,1... | collective-permute-start | bytes 221192 | tf_op jit(solution)/shard_map/ppermute | solution.py:14
  97.5 0.8 copy.460
  98.2 0.8 copy.461
  99.0 0.6 copy.459
  99.6 0.6 copy.462
  100.4 0.8 copy.443
  101.2 0.7 copy.450
  101.8 1.3 reduce.20
  103.2 2.1 %reshape.850 = f32[768,4,24]{2,1,0:T(4,128)S(1)} reshape(f32[32,2304]{1,0:T(8,128)S(1)} %reduce.20) | data formatting | bytes 589824
  105.2 0.9 copy.464
  106.1 0.9 all_to_all.45
  107.0 1.8 %fusion.50 = (f32[4,24,768]{2,1,0:T(8,128)S(1)}, f32[4,24,768]{2,1,0:T(8,128)S(1)}) fusion(f32[4,24,768]{2,1,0:T(8,128)S(1)} %all_to_all.45, f32[4,24,767]{2,1,0:T(8,128)} %copy.461, f32[4,24,1]{2,1,0:T(8,128)} %copy.462, f32[4,24,1]{2,1,0:T(8,128)} %copy.459, f32[4,24,767]{2,1,0:T(8,128)} %copy.460, f32[4,24,768]{2,0,1:T(4,128)S(1)} %bitcast.81), kind=kLoop, calls=%fused_computation.75 | loop fusion | flops 4055040 | bytes 1769472 | tf_op jit(solution)/shard_map/mul | solution.py:68
  108.8 2.0 %fusion.28 = (f32[4,24,768]{2,1,0:T(8,128)S(1)}, f32[4,24,768]{2,1,0:T(8,128)S(1)}, f32[4,24,768]{2,1,0:T(8,128)S(1)}, f32[4,24,768]{2,1,0:T(8,128)S(1)}, f32[4,24,768]{2,1,0:T(8,128)S(1)}) fusion(f32[4,24,768]{2,1,0:T(8,128)S(1)} %all_to_all.45, f32[4,24,768]{2,1,0:T(8,128)S(1)} %get-tuple-element.119), kind=kLoop, calls=%fused_computation.53 | loop fusion | flops 15482880 | bytes 2064384 | tf_op jit(solution)/shard_map/mul | solution.py:68
  111.5 1.1 fusion.53
  115.2 5.6 %collective-permute-start.4 = (f32[3,24,768]{2,1,0:T(8,128)S(1)}, f32[3,24,768]{2,1,0:T(8,128)S(1)}, u32[]{:S(2)}, u32[]{:S(2)}) collective-permute-start(f32[3,24,768]{2,1,0:T(8,128)S(1)} %slice.519), channel_id=1, source_target_pairs={{0,1},{1,2},{2,3},{3,4},{4,5},{5,6},{6,7},{7,8},{8,9},{9,10},{10,1... | collective-permute-start | bytes 663560 | tf_op jit(solution)/shard_map/ppermute | solution.py:14
  120.8 2.8 %collective-permute-done.4 = f32[3,24,768]{2,1,0:T(8,128)S(1)} collective-permute-done((f32[3,24,768]{2,1,0:T(8,128)S(1)}, f32[3,24,768]{2,1,0:T(8,128)S(1)}, u32[]{:S(2)}, u32[]{:S(2)}) %collective-permute-start.4) | collective-permute-done | bytes 221216 | tf_op jit(solution)/shard_map/ppermute | solution.py:14
  123.7 1.9 %collective-permute-start.5 = (f32[3,24,768]{2,1,0:T(8,128)S(1)}, f32[3,24,768]{2,1,0:T(8,128)S(1)}, u32[]{:S(2)}, u32[]{:S(2)}) collective-permute-start(f32[3,24,768]{2,1,0:T(8,128)S(1)} %get-tuple-element.122), channel_id=1, source_target_pairs={{1,0},{2,1},{3,2},{4,3},{5,4},{6,5},{7,6},{8,7},{9,8},{10,9},{11,1... | collective-permute-start | bytes 663560 | tf_op jit(solution)/shard_map/ppermute | solution.py:15
  125.6 10.0 %collective-permute-done.5 = f32[3,24,768]{2,1,0:T(8,128)S(1)} collective-permute-done((f32[3,24,768]{2,1,0:T(8,128)S(1)}, f32[3,24,768]{2,1,0:T(8,128)S(1)}, u32[]{:S(2)}, u32[]{:S(2)}) %collective-permute-start.5) | collective-permute-done | bytes 221216 | tf_op jit(solution)/shard_map/ppermute | solution.py:15
  135.6 1.7 %fusion.226 = f32[4,24,768]{2,1,0:T(8,128)} fusion(f32[4,24,768]{2,1,0:T(8,128)} %copy-done.2, f32[3,24,768]{2,1,0:T(8,128)S(1)} %collective-permute-done.5), kind=kLoop, calls=%fused_computation.310 | loop fusion | flops 55296 | bytes 663552 | tf_op jit(solution)/shard_map/scatter-add | solution.py:83
  (80 shorter events, 8.0 us)
Async XLA Ops:
  24.3 18.0 %collective-permute-start = (f32[1,4,1,256]{3,2,1,0:T(1,128)S(1)}, f32[1,4,1,256]{3,2,1,0:T(1,128)S(1)}, u32[]{:S(2)}, u32[]{:S(2)}) collective-permute-start(f32[1,4,1,256]{3,2,1,0:T(1,128)S(1)} %slice.470), channel_id=1, source_target_pairs={{16,0},{32,16},{48,32},{64,48},{80,64},{96,80},{112,96},{128,112},... | collective-permute-start | bytes 12296 | tf_op jit(solution)/shard_map/ppermute | solution.py:23
  38.4 13.5 %all-to-all-start.2 = ((f32[32,1,512]{2,1,0:T(1,128)}), f32[32,1,512]{2,1,0:T(1,128)S(1)}, u32[]{:S(2)}, u32[]{:S(2)}) async-start(f32[32,1,512]{2,1,0:T(1,128)} %reshape.851), calls=%async_computation.2 | async-start | bytes 131072 | tf_op jit(solution)/shard_map/all_to_all | solution.py:99
  42.6 1.9 %copy-start = (f32[4,24,768]{2,1,0:T(8,128)S(1)}, f32[4,24,768]{2,1,0:T(8,128)}, u32[]{:S(2)}) copy-start(f32[4,24,768]{2,1,0:T(8,128)} %param.20) | copy-start | bytes 884740
  51.9 49.9 %all-to-all-start.1 = ((f32[32,1,2304]{2,1,0:T(1,128)}), f32[32,1,2304]{2,1,0:T(1,128)S(1)}, u32[]{:S(2)}, u32[]{:S(2)}) async-start(f32[32,1,2304]{2,1,0:T(1,128)} %reshape.849), calls=%async_computation.1 | async-start | bytes 589824 | tf_op jit(solution)/shard_map/all_to_all | solution.py:97
  70.0 16.1 %collective-permute-start.1 = (f32[2,4,1,768]{3,1,2,0:T(4,128)S(1)}, f32[2,4,1,768]{3,1,2,0:T(4,128)S(1)}, u32[]{:S(2)}, u32[]{:S(2)}) collective-permute-start(f32[2,4,1,768]{3,1,2,0:T(4,128)S(1)} %copy.428), channel_id=1, source_target_pairs={{16,0},{32,16},{48,32},{64,48},{80,64},{96,80},{112,96},{128,112},... | collective-permute-start | bytes 73736 | tf_op jit(solution)/shard_map/ppermute | solution.py:23
  87.6 13.6 %collective-permute-start.2 = (f32[1,24,768]{2,0,1:T(1,128)S(1)}, f32[1,24,768]{2,0,1:T(1,128)S(1)}, u32[]{:S(2)}, u32[]{:S(2)}) collective-permute-start(f32[1,24,768]{2,0,1:T(1,128)S(1)} %bitcast.98), channel_id=1, source_target_pairs={{1,0},{2,1},{3,2},{4,3},{5,4},{6,5},{7,6},{8,7},{9,8},{10,9},{11,1... | collective-permute-start | bytes 221192 | tf_op jit(solution)/shard_map/ppermute | solution.py:15
  91.6 9.6 %collective-permute-start.3 = (f32[1,24,768]{2,0,1:T(1,128)S(1)}, f32[1,24,768]{2,0,1:T(1,128)S(1)}, u32[]{:S(2)}, u32[]{:S(2)}) collective-permute-start(f32[1,24,768]{2,0,1:T(1,128)S(1)} %bitcast.99), channel_id=1, source_target_pairs={{0,1},{1,2},{2,3},{3,4},{4,5},{5,6},{6,7},{7,8},{8,9},{9,10},{10,1... | collective-permute-start | bytes 221192 | tf_op jit(solution)/shard_map/ppermute | solution.py:14
  107.0 4.5 %copy-start.1 = (f32[4,24,768]{2,1,0:T(8,128)S(1)}, f32[4,24,768]{2,1,0:T(8,128)}, u32[]{:S(2)}) copy-start(f32[4,24,768]{2,1,0:T(8,128)} %copy.443) | copy-start | bytes 884740
  107.0 4.5 %copy-start.3 = (f32[1,24,768]{2,1,0:T(8,128)S(1)}, f32[1,24,768]{2,1,0:T(8,128)}, u32[]{:S(2)}) copy-start(f32[1,24,768]{2,1,0:T(8,128)} %copy.450) | copy-start | bytes 221188
  115.2 8.4 %collective-permute-start.4 = (f32[3,24,768]{2,1,0:T(8,128)S(1)}, f32[3,24,768]{2,1,0:T(8,128)S(1)}, u32[]{:S(2)}, u32[]{:S(2)}) collective-permute-start(f32[3,24,768]{2,1,0:T(8,128)S(1)} %slice.519), channel_id=1, source_target_pairs={{0,1},{1,2},{2,3},{3,4},{4,5},{5,6},{6,7},{7,8},{8,9},{9,10},{10,1... | collective-permute-start | bytes 663560 | tf_op jit(solution)/shard_map/ppermute | solution.py:14
  123.7 11.9 %copy-start.2 = (f32[4,24,768]{2,1,0:T(8,128)}, f32[4,24,768]{2,1,0:T(8,128)S(1)}, u32[]{:S(2)}) copy-start(f32[4,24,768]{2,1,0:T(8,128)S(1)} %get-tuple-element.123) | copy-start | bytes 884740
  123.7 11.9 %collective-permute-start.5 = (f32[3,24,768]{2,1,0:T(8,128)S(1)}, f32[3,24,768]{2,1,0:T(8,128)S(1)}, u32[]{:S(2)}, u32[]{:S(2)}) collective-permute-start(f32[3,24,768]{2,1,0:T(8,128)S(1)} %get-tuple-element.122), channel_id=1, source_target_pairs={{1,0},{2,1},{3,2},{4,3},{5,4},{6,5},{7,6},{8,7},{9,8},{10,9},{11,1... | collective-permute-start | bytes 663560 | tf_op jit(solution)/shard_map/ppermute | solution.py:15
where the time goes:
time: 138 us; the launch traced here: 137 us
  starting transfers between devices  48.5 us (35%)
  local copies, waits for them, and re-layouts  37.4 us (27%)
  blocking collectives  20.6 us (15%)
  other arithmetic  17.3 us (13%)
  waiting for transfers between devices  12.8 us (9%)
    all_to_all x1, blocking collectives, local(): lax.all_to_all(velocity, 'gz', split_axis=1, concat_axis=3, tiled=True)  20.6 us
    ppermute x2, starting transfers between devices, passed_along(): return lax.ppermute(block, axis, route)  18 us
    unnamed x19, local copies, waits for them, and re-layouts  12.5 us
    ppermute x2, starting transfers between devices, padded_2(): before = lax.ppermute(last, axis, up)  11.2 us
    ppermute x2, waiting for transfers between devices, padded_2(): after = lax.ppermute(initial, axis, down)  9.98 us
    all_to_all x1, starting transfers between devices, local(): lax.all_to_all(turned, 'gy', split_axis=1, concat_axis=2, tiled=True)  9.69 us
    concatenate x3, local copies, waits for them, and re-layouts, local(): jnp.concatenate([y_refined[:, :, 1:, :], next_col], axis=2)  7.12 us
    mul x4, other arithmetic, sweep_periodic(): field * kernel_weight(offset - moved)  6.38 us
  transfers between devices with their start and end apart: 8, of which 2 were waited for; matrix products, arithmetic and copies ran while one was open for 26% of the time, Pallas kernels for 0%

commit v1 on v0

v1 whole, which is shorter than its diff:
```python
import jax
import jax.numpy as jnp
from jax import lax
from jax.experimental import pallas as pl
from jax.experimental.pallas import tpu as pltpu
from jax.sharding import PartitionSpec as P

F32 = jnp.float32
BF16 = jnp.bfloat16


def iota(shape, dim):
    return lax.broadcasted_iota(jnp.int32, shape, dim)


def remesh_terms(u, before, after, q):
    up = u >= 0.0
    size = jnp.abs(u)
    a = size - (0.5 * size) * (size - jnp.where(up, after, -before))
    b = a - 0.5
    s = b * b
    e1 = (-1.0 / 16.0 * s + 13.0 / 32.0) * s - 25.0 / 256.0
    e2 = (1.0 / 48.0 * s - 5.0 / 96.0) * s + 3.0 / 256.0
    e0 = 0.5 - e1 - e2
    o0 = ((-25.0 / 12.0 * s + 19.0 / 8.0) * s - 281.0 / 192.0) * b
    o1 = ((25.0 / 24.0 * s - 53.0 / 48.0) * s + 27.0 / 128.0) * b
    o2 = ((-5.0 / 24.0 * s + 3.0 / 16.0) * s - 13.0 / 384.0) * b
    at0 = q * (e0 + o0)
    near1, far1 = q * (e0 - o0), q * (e1 + o1)
    near2, far2 = q * (e1 - o1), q * (e2 + o2)
    near3 = q * (e2 - o2)
    zero = jnp.zeros_like(q)
    return {
        0: at0,
        1: jnp.where(up, near1, far1),
        -1: jnp.where(up, far1, near1),
        2: jnp.where(up, near2, far2),
        -2: jnp.where(up, far2, near2),
        3: jnp.where(up, near3, zero),
        -3: jnp.where(up, zero, near3),
    }


def roll(x, shift, axis):
    n = x.shape[axis]
    shift = shift % n
    return x if shift == 0 else pltpu.roll(x, shift, axis)


def sweep_ring(q, u, axis):
    terms = remesh_terms(u, roll(u, 1, axis), roll(u, -1, axis), q)
    total = terms[0]
    for m in (1, -1, 2, -2, 3, -3):
        total = total + roll(terms[m], m, axis)
    return total


def pack_velocity(v_ref, out_ref):
    blank = jnp.zeros((8, 16), F32)
    for k in range(16):
        planes = [v_ref[c, 4 * k + p] for c in range(2) for p in range(4)]
        out_ref[k, 0:8, :] = jnp.concatenate(planes, axis=1)
        planes = [v_ref[2, z] if 0 <= z < 64 else blank for z in range(4 * k - 1, 4 * k + 5)]
        out_ref[k, 8:16, :] = jnp.concatenate(planes + [blank, blank], axis=1)


def pack_scalar(s_ref, out_ref, t_ref):
    for v in range(6):
        block = s_ref[:, :, 128 * v : 128 * v + 128].reshape(96, 128)
        block = jnp.concatenate([block, jnp.zeros((32, 128), F32)], axis=0)
        t_ref[128 * v : 128 * v + 128, :] = block.T
    lane = iota((8, 128), 1)
    row = iota((8, 128), 0)
    for i in range(32):
        left = t_ref[(24 * i - 8) % 768 : (24 * i - 8) % 768 + 8, :]
        right = t_ref[(24 * i + 24) % 768 : (24 * i + 24) % 768 + 8, :]
        halo = jnp.where(row < 4, right, left)
        for t in range(3):
            tile = t_ref[24 * i + 8 * t : 24 * i + 8 * t + 8, :]
            out_ref[i, 8 * t : 8 * t + 8, :] = jnp.where(lane < 96, tile, roll(halo, 96 - 32 * t, 1))


def spread_velocity(r_ref, out_ref):
    col = iota((8, 128), 1) & 15
    for i in range(32):
        k = i // 2
        for g in range(2):
            here = r_ref[k, 8 * g : 8 * g + 8, :]
            if i % 2 == 0:
                other = r_ref[(k - 1) % 16, 8 * g : 8 * g + 8, :]
                tile = jnp.where(col == 0, roll(other, -15, 1), roll(here, 1, 1))
            else:
                other = r_ref[(k + 1) % 16, 8 * g : 8 * g + 8, :]
                tile = jnp.where(col < 9, roll(here, -7, 1), roll(other, 9, 1))
            out_ref[i, 8 * g : 8 * g + 8, :] = tile


def pieces(x):
    hi = x.astype(BF16)
    rest = x - hi.astype(F32)
    mid = rest.astype(BF16)
    return hi, mid, (rest - mid.astype(F32)).astype(BF16)


def split_dot(left, right, split_left):
    total = None
    for part in pieces(left if split_left else right)[::-1]:
        pair = (part, right) if split_left else (left, part)
        term = jnp.dot(*pair, preferred_element_type=F32)
        total = term if total is None else total + term
    return total


def hat_rows(rows, slot, ring):
    e = iota((rows, 128), 0)
    if ring:
        e = jnp.where(e > 28, e - 32, e)
    lane = iota((rows, 128), 1)
    away = jnp.abs(e - 3 * ((lane & 15) - 1))
    return jnp.where((lane >> 4) == slot, jnp.maximum(3 - away, 0), 0).astype(F32).astype(BF16)


def sweeps(s_ref, v_ref, own_ref, up_ref, down_ref, my_ref, f_ref, ux_ref, uy_ref, uz_ref, x_ref, y_ref):
    for v in range(6):
        c = iota((256, 128), 0)
        f = iota((256, 128), 1) + 128 * v
        away = jnp.abs(f - 3 * c)
        away = jnp.minimum(away, 768 - away)
        my_ref[:, 128 * v : 128 * v + 128] = jnp.maximum(3 - away, 0).astype(F32).astype(BF16)
    my = my_ref[...]
    xy = jnp.concatenate([hat_rows(32, p, True) for p in range(4)] + [hat_rows(24, 4 + p, False) for p in range(4)], axis=0)
    zz = jnp.concatenate([hat_rows(24, p, False) for p in range(6)], axis=0)
    for g in range(2):
        coarse = v_ref[:, 8 * g : 8 * g + 8, :].reshape(256, 128)
        fine_y = split_dot(coarse.T, my, True)
        fine = split_dot(xy if g == 0 else zz, fine_y, False) * (1.0 / 9.0)
        if g == 0:
            ux_ref[...] = fine[:128].reshape(4, 32, 768)
            uy_ref[...] = fine[128:].reshape(4, 24, 768)
        else:
            uz_ref[...] = fine.reshape(6, 24, 768)
    lane = iota((8, 128), 1)
    for i in range(32):
        tiles = [s_ref[i, 8 * t : 8 * t + 8, :] for t in range(3)]
        halo = jnp.where(lane < 32, roll(tiles[0], -96, 1), jnp.where(lane < 64, roll(tiles[1], -64, 1), roll(tiles[2], -32, 1)))
        for t, tile in enumerate(tiles + [halo]):
            for p in range(4):
                v, at = divmod(24 * i, 128)
                moved = roll(tile, at - 24 * p, 1)
                here = min(24, 128 - at)
                f_ref[p, 8 * t : 8 * t + 8, 128 * v + at : 128 * v + at + here] = moved[:, at : at + here]
                if here < 24:
                    f_ref[p, 8 * t : 8 * t + 8, 128 * v + 128 : 128 * v + 128 + 24 - here] = moved[:, : 24 - here]
    for p in range(4):
        for v in range(6):
            part = slice(128 * v, 128 * v + 128)
            x_ref[p, :, part] = sweep_ring(f_ref[p, :, part], ux_ref[p, :, part], 0)[:24]
    for p in range(4):
        for t in range(3):
            rows = slice(8 * t, 8 * t + 8)
            y_ref[p, rows, :] = sweep_ring(x_ref[p, rows, :], uy_ref[p, rows, :], 1)
    for t in range(3):
        rows = slice(8 * t, 8 * t + 8)
        for v in range(6):
            part = slice(128 * v, 128 * v + 128)
            speeds = [uz_ref[p, rows, part] for p in range(6)]
            total = {}
            for p in range(4):
                terms = remesh_terms(speeds[p + 1], speeds[p], speeds[p + 2], y_ref[p, rows, part])
                for m, term in terms.items():
                    total[p + m] = total[p + m] + term if p + m in total else term
            for j in range(3):
                down_ref[j, rows, part] = total[j - 3]
                up_ref[j, rows, part] = total[j + 4]
            for j in range(4):
                own_ref[j, rows, part] = total[j]


def join(own_ref, low_ref, high_ref, out_ref):
    out_ref[0] = own_ref[0] + low_ref[0]
    out_ref[1] = own_ref[1] + low_ref[1] + high_ref[0]
    out_ref[2] = own_ref[2] + low_ref[2] + high_ref[1]
    out_ref[3] = own_ref[3] + high_ref[2]


def kernel(body, *shapes, scratch=()):
    outs = tuple(jax.ShapeDtypeStruct(s, F32) for s in shapes)
    return pl.pallas_call(
        body,
        out_shape=outs if len(outs) > 1 else outs[0],
        scratch_shapes=[pltpu.VMEM(s, d) for s, d in scratch],
    )


def exchange(x, axis):
    return lax.all_to_all(x, axis, split_axis=0, concat_axis=0, tiled=False)


def local(scalar, velocity):
    chunks = kernel(pack_velocity, (16, 16, 128))(velocity)
    planes = exchange(chunks, "gz")
    field = exchange(kernel(pack_scalar, (32, 24, 128), scratch=[((768, 128), F32)])(scalar), "gy")
    speeds = exchange(kernel(spread_velocity, (32, 16, 128))(planes), "gy")
    own, up, down = kernel(
        sweeps,
        (4, 24, 768),
        (3, 24, 768),
        (3, 24, 768),
        scratch=[
            ((256, 768), BF16),
            ((4, 32, 768), F32),
            ((4, 32, 768), F32),
            ((4, 24, 768), F32),
            ((6, 24, 768), F32),
            ((4, 24, 768), F32),
            ((4, 24, 768), F32),
        ],
    )(field, speeds)
    steps = [(k, k + 1) for k in range(lax.axis_size("gz") - 1)]
    low = lax.ppermute(up, "gz", steps)
    high = lax.ppermute(down, "gz", [(b, a) for a, b in steps])
    return kernel(join, (4, 24, 768))(own, low, high)


def solution(mesh):
    in_specs = (P("gz", "gy", None), P(None, None, "gy", "gz"))
    out_specs = P("gz", "gy", None)
    return jax.shard_map(local, mesh=mesh, in_specs=in_specs, out_specs=out_specs, check_vma=False)
```

time: 138 us -> 98.8 us (0.72)
  the two profiles are of different devices: /device:TPU:1 before, /device:TPU:57 now
where the time goes in v1:
time: 98.8 us; the launch traced here: 98.2 us
  blocking collectives  34.5 us (35%)
  starting transfers between devices  24.4 us (25%)
  waiting for transfers between devices  21.7 us (22%)
  Pallas kernels  14.8 us (15%)
  local copies, waits for them, and re-layouts  2.8 us (3%)
    all_to_all x2, blocking collectives, exchange(): return lax.all_to_all(x, axis, split_axis=0, concat_axis=0, tiled=False)  34.5 us
    all_to_all x1, starting transfers between devices, exchange(): return lax.all_to_all(x, axis, split_axis=0, concat_axis=0, tiled=False)  14.2 us
    ppermute x1, waiting for transfers between devices, local(): high = lax.ppermute(down, 'gz', [(b, a) for a, b in steps])  11.3 us
    all_to_all x1, waiting for transfers between devices, exchange(): return lax.all_to_all(x, axis, split_axis=0, concat_axis=0, tiled=False)  8.93 us
    ppermute x1, starting transfers between devices, local(): low = lax.ppermute(up, 'gz', steps)  8.35 us
    pallas_call x1, Pallas kernels, local(): kernel(sweeps, (4, 24, 768), (3, 24, 768), (3, 24, 768), scratch=[((256,...  7 us
    unnamed x7, local copies, waits for them, and re-layouts  2.8 us
    pallas_call x1, Pallas kernels, local(): kernel(pack_scalar, (32, 24, 128), scratch=[((768, 128), F32)])(scalar)  2.06 us
  transfers between devices with their start and end apart: 3, of which 3 were waited for; matrix products, arithmetic and copies ran while one was open for 0% of the time, Pallas kernels for 2%

profile of v1, /device:TPU:57, one launch (start us, length us, event | category | flops | bytes accessed | tf_op | source)
XLA Modules:
  0.0 98.2 jit_solution(1280816972098105276)
XLA Ops:
  0.0 2.1 %copy.3.v_ref = f32[3,64,8,16]{3,2,1,0:T(8,128)} copy(f32[3,64,8,16]{1,3,2,0:T(8,128)} %param.3) | data formatting | bytes 196608 | tf_op args[1]
  2.1 2.1 %shard_map.29 = f32[16,16,128]{2,1,0:T(8,128)} custom-call(f32[3,64,8,16]{3,2,1,0:T(8,128)} %copy.3.v_ref), custom_call_target="tpu_custom_call" | custom-call | tf_op jit(solution)/shard_map/pallas_call | solution.py:200
  4.1 15.3 %all_to_all.15.r_ref = f32[16,16,128]{2,1,0:T(8,128)} all-to-all(f32[16,16,128]{2,1,0:T(8,128)} %shard_map.29), channel_id=1, replica_groups=mesh['gy'=32,'gz'=16] {'gz'}, dimensions={0} | all-to-all | bytes 262144 | tf_op jit(solution)/shard_map/all_to_all | solution.py:196
  19.5 1.8 %shard_map.30 = f32[32,16,128]{2,1,0:T(8,128)} custom-call(f32[16,16,128]{2,1,0:T(8,128)} %all_to_all.15.r_ref), custom_call_target="tpu_custom_call" | custom-call | tf_op jit(solution)/shard_map/pallas_call | solution.py:203
  21.3 14.2 %all-to-all-start.2 = ((f32[32,16,128]{2,1,0:T(8,128)}), f32[32,16,128]{2,1,0:T(8,128)S(1)}, u32[]{:S(2)}, u32[]{:S(2)}) async-start(f32[32,16,128]{2,1,0:T(8,128)} %shard_map.30), calls=%async_computation.2 | async-start | bytes 524288 | tf_op jit(solution)/shard_map/all_to_all | solution.py:196
  35.4 2.1 %shard_map.28 = f32[32,24,128]{2,1,0:T(8,128)} custom-call(f32[4,24,768]{2,1,0:T(8,128)} %s_ref.1), custom_call_target="tpu_custom_call" | custom-call | tf_op jit(solution)/shard_map/pallas_call | solution.py:202
  37.5 8.9 %all-to-all-done.2.v_ref = f32[32,16,128]{2,1,0:T(8,128)S(1)} async-done(((f32[32,16,128]{2,1,0:T(8,128)}), f32[32,16,128]{2,1,0:T(8,128)S(1)}, u32[]{:S(2)}, u32[]{:S(2)}) %all-to-all-start.2) | async-done | bytes 262176 | tf_op jit(solution)/shard_map/all_to_all | solution.py:196
  46.4 0.0 copy-start
  46.4 19.2 %all_to_all.16.s_ref = f32[32,24,128]{2,1,0:T(8,128)} all-to-all(f32[32,24,128]{2,1,0:T(8,128)} %shard_map.28), channel_id=1, replica_groups=mesh['gy'=32,'gz'=16] {'gy'}, dimensions={0} | all-to-all | bytes 786432 | tf_op jit(solution)/shard_map/all_to_all | solution.py:196
  65.6 0.0 copy-done
  65.6 7.0 %shard_map.31 = (f32[4,24,768]{2,1,0:T(8,128)}, f32[3,24,768]{2,1,0:T(8,128)}, f32[3,24,768]{2,1,0:T(8,128)}) custom-call(f32[32,24,128]{2,1,0:T(8,128)} %all_to_all.16.s_ref, f32[32,16,128]{2,1,0:T(8,128)} %copy-done), custom_call_target="tpu_custom_call" | custom-call | tf_op jit(solution)/shard_map/pallas_call | solution.py:204
  72.6 8.3 %collective-permute-start = (f32[3,24,768]{2,1,0:T(8,128)}, f32[3,24,768]{2,1,0:T(8,128)S(1)}, u32[]{:S(2)}, u32[]{:S(2)}) collective-permute-start(f32[3,24,768]{2,1,0:T(8,128)} %get-tuple-element.9), channel_id=1, source_target_pairs={{0,1},{1,2},{2,3},{3,4},{4,5},{5,6},{6,7},{7,8},{8,9},{9,10},{10,1... | collective-permute-start | bytes 663560 | tf_op jit(solution)/shard_map/ppermute | solution.py:220
  81.0 1.9 %collective-permute-start.1 = (f32[3,24,768]{2,1,0:T(8,128)}, f32[3,24,768]{2,1,0:T(8,128)S(1)}, u32[]{:S(2)}, u32[]{:S(2)}) collective-permute-start(f32[3,24,768]{2,1,0:T(8,128)} %get-tuple-element.10), channel_id=1, source_target_pairs={{1,0},{2,1},{3,2},{4,3},{5,4},{6,5},{7,6},{8,7},{9,8},{10,9},{11,1... | collective-permute-start | bytes 663560 | tf_op jit(solution)/shard_map/ppermute | solution.py:221
  82.9 1.4 %collective-permute-done.low_ref = f32[3,24,768]{2,1,0:T(8,128)S(1)} collective-permute-done((f32[3,24,768]{2,1,0:T(8,128)}, f32[3,24,768]{2,1,0:T(8,128)S(1)}, u32[]{:S(2)}, u32[]{:S(2)}) %collective-permute-start) | collective-permute-done | bytes 221216 | tf_op jit(solution)/shard_map/ppermute | solution.py:220
  84.3 0.0 copy-start.1
  84.3 11.3 %collective-permute-done.1.high_ref = f32[3,24,768]{2,1,0:T(8,128)S(1)} collective-permute-done((f32[3,24,768]{2,1,0:T(8,128)}, f32[3,24,768]{2,1,0:T(8,128)S(1)}, u32[]{:S(2)}, u32[]{:S(2)}) %collective-permute-start.1) | collective-permute-done | bytes 221216 | tf_op jit(solution)/shard_map/ppermute | solution.py:221
  95.6 0.0 copy-start.2
  95.6 0.0 copy-done.1
  95.6 0.7 copy-done.2
  96.3 1.9 %shard_map.32 = f32[4,24,768]{2,1,0:T(8,128)} custom-call(f32[4,24,768]{2,1,0:T(8,128)} %get-tuple-element.8.own_ref, f32[3,24,768]{2,1,0:T(8,128)} %copy-done.1, f32[3,24,768]{2,1,0:T(8,128)} %copy-done.2), custom_call_target="tpu_custom_call" | custom-call | tf_op jit(solution)/shard_map/pallas_call | solution.py:222
Async XLA Ops:
  21.3 25.2 %all-to-all-start.2 = ((f32[32,16,128]{2,1,0:T(8,128)}), f32[32,16,128]{2,1,0:T(8,128)S(1)}, u32[]{:S(2)}, u32[]{:S(2)}) async-start(f32[32,16,128]{2,1,0:T(8,128)} %shard_map.30), calls=%async_computation.2 | async-start | bytes 524288 | tf_op jit(solution)/shard_map/all_to_all | solution.py:196
  46.4 19.2 %copy-start = (f32[32,16,128]{2,1,0:T(8,128)}, f32[32,16,128]{2,1,0:T(8,128)S(1)}, u32[]{:S(2)}) copy-start(f32[32,16,128]{2,1,0:T(8,128)S(1)} %all-to-all-done.2.v_ref) | copy-start | bytes 786436
  72.6 11.7 %collective-permute-start = (f32[3,24,768]{2,1,0:T(8,128)}, f32[3,24,768]{2,1,0:T(8,128)S(1)}, u32[]{:S(2)}, u32[]{:S(2)}) collective-permute-start(f32[3,24,768]{2,1,0:T(8,128)} %get-tuple-element.9), channel_id=1, source_target_pairs={{0,1},{1,2},{2,3},{3,4},{4,5},{5,6},{6,7},{7,8},{8,9},{9,10},{10,1... | collective-permute-start | bytes 663560 | tf_op jit(solution)/shard_map/ppermute | solution.py:220
  81.0 14.7 %collective-permute-start.1 = (f32[3,24,768]{2,1,0:T(8,128)}, f32[3,24,768]{2,1,0:T(8,128)S(1)}, u32[]{:S(2)}, u32[]{:S(2)}) collective-permute-start(f32[3,24,768]{2,1,0:T(8,128)} %get-tuple-element.10), channel_id=1, source_target_pairs={{1,0},{2,1},{3,2},{4,3},{5,4},{6,5},{7,6},{8,7},{9,8},{10,9},{11,1... | collective-permute-start | bytes 663560 | tf_op jit(solution)/shard_map/ppermute | solution.py:221
  84.3 11.3 %copy-start.1 = (f32[3,24,768]{2,1,0:T(8,128)}, f32[3,24,768]{2,1,0:T(8,128)S(1)}, u32[]{:S(2)}) copy-start(f32[3,24,768]{2,1,0:T(8,128)S(1)} %collective-permute-done.low_ref) | copy-start | bytes 663556
  95.6 0.7 copy-start.2

commit v2 on v1

--- a/solution.py
+++ b/solution.py
@@ -55,44 +55,74 @@
     return total
 
 
+def swap_blocks(x):
+    row = iota((8, 128), 0)
+    block = iota((8, 128), 1) >> 4
+    for bit in (1, 2, 4):
+        low = (row & bit) == 0
+        first = (block & bit) == 0
+        upward = roll(roll(x, -bit, 0), 16 * bit, 1)
+        downward = roll(roll(x, bit, 0), -16 * bit, 1)
+        x = jnp.where(low == first, x, jnp.where(low, upward, downward))
+    return x
+
+
 def pack_velocity(v_ref, out_ref):
-    blank = jnp.zeros((8, 16), F32)
+    lane = iota((8, 128), 1)
+    tiles = []
+    for c in range(3):
+        block = v_ref[c].reshape(128, 64)
+        block = jnp.concatenate([block, jnp.zeros((128, 64), F32)], axis=1).T
+        tiles.append([swap_blocks(block[8 * n : 8 * n + 8]) for n in range(8)])
+    zero = jnp.zeros((8, 128), F32)
     for k in range(16):
-        planes = [v_ref[c, 4 * k + p] for c in range(2) for p in range(4)]
-        out_ref[k, 0:8, :] = jnp.concatenate(planes, axis=1)
-        planes = [v_ref[2, z] if 0 <= z < 64 else blank for z in range(4 * k - 1, 4 * k + 5)]
-        out_ref[k, 8:16, :] = jnp.concatenate(planes + [blank, blank], axis=1)
-
-
-def pack_scalar(s_ref, out_ref, t_ref):
+        n, odd = divmod(k, 2)
+        if odd == 0:
+            out_ref[k, 0:8, :] = jnp.where(lane < 64, tiles[0][n], roll(tiles[1][n], 64, 1))
+            before = tiles[2][n - 1] if n > 0 else zero
+            planes = jnp.where(lane < 16, roll(before, 16, 1), roll(tiles[2][n], 16, 1))
+        else:
+            out_ref[k, 0:8, :] = jnp.where(lane < 64, roll(tiles[0][n], -64, 1), tiles[1][n])
+            after = tiles[2][n + 1] if n < 7 else zero
+            planes = jnp.where(lane < 80, roll(tiles[2][n], -48, 1), roll(after, 80, 1))
+        out_ref[k, 8:16, :] = jnp.where(lane < 96, planes, zero)
+
+
+def pack_chunks(s_ref, r_ref, out_ref, t_ref):
     for v in range(6):
         block = s_ref[:, :, 128 * v : 128 * v + 128].reshape(96, 128)
         block = jnp.concatenate([block, jnp.zeros((32, 128), F32)], axis=0)
         t_ref[128 * v : 128 * v + 128, :] = block.T
     lane = iota((8, 128), 1)
     row = iota((8, 128), 0)
+    col = lane & 15
+    slot = lane >> 4
     for i in range(32):
+        k = i // 2
+        here, depth = r_ref[k, 0:8, :], r_ref[k, 8:16, :]
+        if i % 2 == 0:
+            other = r_ref[(k - 1) % 16, 0:8, :]
+            wide = jnp.where(col == 0, roll(other, -15, 1), roll(here, 1, 1))
+            near = here
+        else:
+            other = r_ref[(k + 1) % 16, 0:8, :]
+            wide = jnp.where(col < 9, roll(here, -7, 1), roll(other, 9, 1))
+            near = jnp.where(col < 8, roll(here, -8, 1), roll(other, 8, 1))
+            depth = jnp.where(col < 8, roll(depth, -8, 1), roll(r_ref[(k + 1) % 16, 8:16, :], 8, 1))
+        tile = jnp.where(slot < 4, wide, near)
+        tile = jnp.where((slot >= 4) & (col >= 9), roll(depth, 73, 1), tile)
+        tile = jnp.where((slot < 2) & (col >= 11), roll(depth, -53, 1), tile)
+        tile = jnp.where(((slot >> 1) == 1) & (col >= 11), roll(depth, -26, 1), tile)
+        out_ref[i, 24:32, :] = tile
+        rest = jnp.where((slot < 4) & ((col == 7) | (col == 8)), depth, 0.0)
+        rest = pltpu.roll(rest, 0, 1, stride=2, stride_axis=0)
+        stash = jnp.sum(rest, axis=0, keepdims=True)
         left = t_ref[(24 * i - 8) % 768 : (24 * i - 8) % 768 + 8, :]
         right = t_ref[(24 * i + 24) % 768 : (24 * i + 24) % 768 + 8, :]
-        halo = jnp.where(row < 4, right, left)
+        halo = jnp.where(row < 3, right, jnp.where(row == 3, stash, left))
         for t in range(3):
             tile = t_ref[24 * i + 8 * t : 24 * i + 8 * t + 8, :]
             out_ref[i, 8 * t : 8 * t + 8, :] = jnp.where(lane < 96, tile, roll(halo, 96 - 32 * t, 1))
-
-
-def spread_velocity(r_ref, out_ref):
-    col = iota((8, 128), 1) & 15
-    for i in range(32):
-        k = i // 2
-        for g in range(2):
-            here = r_ref[k, 8 * g : 8 * g + 8, :]
-            if i % 2 == 0:
-                other = r_ref[(k - 1) % 16, 8 * g : 8 * g + 8, :]
-                tile = jnp.where(col == 0, roll(other, -15, 1), roll(here, 1, 1))
-            else:
-                other = r_ref[(k + 1) % 16, 8 * g : 8 * g + 8, :]
-                tile = jnp.where(col < 9, roll(here, -7, 1), roll(other, 9, 1))
-            out_ref[i, 8 * g : 8 * g + 8, :] = tile
 
 
 def pieces(x):
@@ -114,32 +144,17 @@
 def hat_rows(rows, slot, ring):
     e = iota((rows, 128), 0)
     if ring:
-        e = jnp.where(e > 28, e - 32, e)
+        e = jnp.where(e > 28, e - 32, e) + 3
     lane = iota((rows, 128), 1)
-    away = jnp.abs(e - 3 * ((lane & 15) - 1))
+    away = jnp.abs(e - 3 * (lane & 15))
     return jnp.where((lane >> 4) == slot, jnp.maximum(3 - away, 0), 0).astype(F32).astype(BF16)
 
 
-def sweeps(s_ref, v_ref, own_ref, up_ref, down_ref, my_ref, f_ref, ux_ref, uy_ref, uz_ref, x_ref, y_ref):
-    for v in range(6):
-        c = iota((256, 128), 0)
-        f = iota((256, 128), 1) + 128 * v
-        away = jnp.abs(f - 3 * c)
-        away = jnp.minimum(away, 768 - away)
-        my_ref[:, 128 * v : 128 * v + 128] = jnp.maximum(3 - away, 0).astype(F32).astype(BF16)
-    my = my_ref[...]
-    xy = jnp.concatenate([hat_rows(32, p, True) for p in range(4)] + [hat_rows(24, 4 + p, False) for p in range(4)], axis=0)
-    zz = jnp.concatenate([hat_rows(24, p, False) for p in range(6)], axis=0)
-    for g in range(2):
-        coarse = v_ref[:, 8 * g : 8 * g + 8, :].reshape(256, 128)
-        fine_y = split_dot(coarse.T, my, True)
-        fine = split_dot(xy if g == 0 else zz, fine_y, False) * (1.0 / 9.0)
-        if g == 0:
-            ux_ref[...] = fine[:128].reshape(4, 32, 768)
-            uy_ref[...] = fine[128:].reshape(4, 24, 768)
-        else:
-            uz_ref[...] = fine.reshape(6, 24, 768)
+def sweeps(s_ref, own_ref, up_ref, down_ref, my_ref, c_ref, f_ref, ux_ref, uy_ref, uz_ref, x_ref, y_ref):
     lane = iota((8, 128), 1)
+    row = iota((8, 128), 0)
+    col = lane & 15
+    slot = lane >> 4
     for i in range(32):
         tiles = [s_ref[i, 8 * t : 8 * t + 8, :] for t in range(3)]
         halo = jnp.where(lane < 32, roll(tiles[0], -96, 1), jnp.where(lane < 64, roll(tiles[1], -64, 1), roll(tiles[2], -32, 1)))
@@ -151,6 +166,30 @@
                 f_ref[p, 8 * t : 8 * t + 8, 128 * v + at : 128 * v + at + here] = moved[:, at : at + here]
                 if here < 24:
                     f_ref[p, 8 * t : 8 * t + 8, 128 * v + 128 : 128 * v + 128 + 24 - here] = moved[:, : 24 - here]
+        packed = s_ref[i, 24:32, :]
+        rest = jnp.broadcast_to(halo[3:4, :], (8, 128))
+        for bit in (1, 2, 4):
+            rest = jnp.where((row & bit) == 0, rest, roll(rest, -2 * bit, 1))
+        depth = jnp.where(slot >= 4, jnp.where(col < 5, roll(packed, 53, 1), roll(packed, 26, 1)), jnp.where(col < 7, roll(packed, -73, 1), rest))
+        c_ref[0, 8 * i : 8 * i + 8, :] = packed
+        c_ref[1, 8 * i : 8 * i + 8, :] = depth
+    for v in range(6):
+        c = iota((256, 128), 0)
+        f = iota((256, 128), 1) + 128 * v
+        away = jnp.abs(f - 3 * c)
+        away = jnp.minimum(away, 768 - away)
+        my_ref[:, 128 * v : 128 * v + 128] = jnp.maximum(3 - away, 0).astype(F32).astype(BF16)
+    my = my_ref[...]
+    xy = jnp.concatenate([hat_rows(32, p, True) for p in range(4)] + [hat_rows(24, 4 + p, False) for p in range(4)], axis=0)
+    zz = jnp.concatenate([hat_rows(24, p, False) for p in range(6)], axis=0)
+    for g in range(2):
+        fine_y = split_dot(c_ref[g].T, my, True)
+        fine = split_dot(xy if g == 0 else zz, fine_y, False) * (1.0 / 9.0)
+        if g == 0:
+            ux_ref[...] = fine[:128].reshape(4, 32, 768)
+            uy_ref[...] = fine[128:].reshape(4, 24, 768)
+        else:
+            uz_ref[...] = fine.reshape(6, 24, 768)
     for p in range(4):
         for v in range(6):
             part = slice(128 * v, 128 * v + 128)
@@ -189,6 +228,7 @@
         body,
         out_shape=outs if len(outs) > 1 else outs[0],
         scratch_shapes=[pltpu.VMEM(s, d) for s, d in scratch],
+        compiler_params=pltpu.CompilerParams(vmem_limit_bytes=16 * 1024 * 1024),
     )
 
 
@@ -197,10 +237,8 @@
 
 
 def local(scalar, velocity):
-    chunks = kernel(pack_velocity, (16, 16, 128))(velocity)
-    planes = exchange(chunks, "gz")
-    field = exchange(kernel(pack_scalar, (32, 24, 128), scratch=[((768, 128), F32)])(scalar), "gy")
-    speeds = exchange(kernel(spread_velocity, (32, 16, 128))(planes), "gy")
+    planes = exchange(kernel(pack_velocity, (16, 16, 128))(jnp.transpose(velocity, (0, 2, 3, 1))), "gz")
+    chunks = exchange(kernel(pack_chunks, (32, 32, 128), scratch=[((768, 128), F32)])(scalar, planes), "gy")
     own, up, down = kernel(
         sweeps,
         (4, 24, 768),
@@ -208,6 +246,7 @@
         (3, 24, 768),
         scratch=[
             ((256, 768), BF16),
+            ((2, 256, 128), F32),
             ((4, 32, 768), F32),
             ((4, 32, 768), F32),
             ((4, 24, 768), F32),
@@ -215,7 +254,7 @@
             ((4, 24, 768), F32),
             ((4, 24, 768), F32),
         ],
-    )(field, speeds)
+    )(chunks)
     steps = [(k, k + 1) for k in range(lax.axis_size("gz") - 1)]
     low = lax.ppermute(up, "gz", steps)
     high = lax.ppermute(down, "gz", [(b, a) for a, b in steps])

time: 98.8 us -> 79.9 us (0.81)
  starting transfers between devices: 24.4 us -> 10.4 us
  blocking collectives: 34.5 us -> 45.2 us
  waiting for transfers between devices: 21.7 us -> 12.5 us
  Pallas kernels: 14.8 us -> 10.5 us
  local copies, waits for them, and re-layouts: 2.8 us -> 0.93 us
    all_to_all x1 -> x0, starting transfers between devices: 14.2 us -> none  [exchange(): return lax.all_to_all(x, axis, split_axis=0, concat_axis=0, tiled=False)]
    all_to_all x2, blocking collectives: 34.5 us -> 45.2 us  [exchange(): return lax.all_to_all(x, axis, split_axis=0, concat_axis=0, tiled=False)]
    all_to_all x1 -> x0, waiting for transfers between devices: 8.93 us -> none  [exchange(): return lax.all_to_all(x, axis, split_axis=0, concat_axis=0, tiled=False)]
    pallas_call x3 -> x2, Pallas kernels: 5.92 us -> 3.56 us  [the longest x1 3.1 us: local(): kernel(pack_chunks, (32, 32, 128), scratch=[((768, 128), F32)])]
    unnamed x7 -> x4, local copies, waits for them, and re-layouts: 2.8 us -> 0.93 us
    pallas_call x1, Pallas kernels: 1.88 us -> 0.77 us  [local(): return kernel(join, (4, 24, 768))(own, low, high)]
  transfers between devices with their start and end apart: 3 -> 2, of which waited for: 3 -> 2; matrix products, arithmetic and copies ran while one was open for 0% -> 0% of each run, Pallas kernels for 2% -> 0%
where the time goes in v2:
time: 79.9 us; the launch traced here: 79.7 us
  blocking collectives  45.2 us (57%)
  waiting for transfers between devices  12.5 us (16%)
  Pallas kernels  10.5 us (13%)
  starting transfers between devices  10.4 us (13%)
  local copies, waits for them, and re-layouts  0.93 us (1%)
    all_to_all x2, blocking collectives, exchange(): return lax.all_to_all(x, axis, split_axis=0, concat_axis=0, tiled=False)  45.2 us
    ppermute x1, waiting for transfers between devices, local(): high = lax.ppermute(down, 'gz', [(b, a) for a, b in steps])  11.4 us
    ppermute x1, starting transfers between devices, local(): low = lax.ppermute(up, 'gz', steps)  8.46 us
    pallas_call x1, Pallas kernels, local(): kernel(sweeps, (4, 24, 768), (3, 24, 768), (3, 24, 768), scratch=[((256,...  6.21 us
    pallas_call x1, Pallas kernels, local(): kernel(pack_chunks, (32, 32, 128), scratch=[((768, 128), F32)])  3.1 us
    ppermute x1, starting transfers between devices, local(): high = lax.ppermute(down, 'gz', [(b, a) for a, b in steps])  1.92 us
  transfers between devices with their start and end apart: 2, of which 2 were waited for; matrix products, arithmetic and copies ran while one was open for 0% of the time, Pallas kernels for 0%

profile of v2, /device:TPU:57, one launch (start us, length us, event | category | flops | bytes accessed | tf_op | source)
XLA Modules:
  0.0 79.7 jit_solution(1364499212268848778)
XLA Ops:
  0.0 0.0 copy-start.1
  0.0 0.9 %copy-done.1 = f32[3,64,8,16]{1,3,2,0:T(8,128)S(1)} copy-done((f32[3,64,8,16]{1,3,2,0:T(8,128)S(1)}, f32[3,64,8,16]{1,3,2,0:T(8,128)}, u32[]{:S(2)}) %copy-start.1) | copy-done | bytes 98328
  0.9 0.0 copy-start
  0.9 0.5 shard_map.28
  1.4 15.0 %all_to_all.10.r_ref = f32[16,16,128]{2,1,0:T(8,128)S(1)} all-to-all(f32[16,16,128]{2,1,0:T(8,128)S(1)} %shard_map.28), channel_id=1, replica_groups=mesh['gy'=32,'gz'=16] {'gz'}, dimensions={0} | all-to-all | bytes 262144 | tf_op jit(solution)/shard_map/all_to_all | solution.py:236
  16.4 0.0 copy-done
  16.4 3.1 %shard_map.29 = f32[32,32,128]{2,1,0:T(8,128)S(1)} custom-call(f32[4,24,768]{2,1,0:T(8,128)S(1)} %copy-done, f32[16,16,128]{2,1,0:T(8,128)S(1)} %all_to_all.10.r_ref), custom_call_target="tpu_custom_call" | custom-call | tf_op jit(solution)/shard_map/pallas_call | solution.py:241
  19.5 30.2 %all_to_all.11.s_ref = f32[32,32,128]{2,1,0:T(8,128)S(1)} all-to-all(f32[32,32,128]{2,1,0:T(8,128)S(1)} %shard_map.29), channel_id=1, replica_groups=mesh['gy'=32,'gz'=16] {'gy'}, dimensions={0} | all-to-all | bytes 1048576 | tf_op jit(solution)/shard_map/all_to_all | solution.py:236
  49.7 6.2 %shard_map.30 = (f32[4,24,768]{2,1,0:T(8,128)S(1)}, f32[3,24,768]{2,1,0:T(8,128)S(1)}, f32[3,24,768]{2,1,0:T(8,128)S(1)}) custom-call(f32[32,32,128]{2,1,0:T(8,128)S(1)} %all_to_all.11.s_ref), custom_call_target="tpu_custom_call" | custom-call | tf_op jit(solution)/shard_map/pallas_call | solution.py:242
  55.9 8.5 %collective-permute-start = (f32[3,24,768]{2,1,0:T(8,128)S(1)}, f32[3,24,768]{2,1,0:T(8,128)S(1)}, u32[]{:S(2)}, u32[]{:S(2)}) collective-permute-start(f32[3,24,768]{2,1,0:T(8,128)S(1)} %get-tuple-element.9), channel_id=1, source_target_pairs={{0,1},{1,2},{2,3},{3,4},{4,5},{5,6},{6,7},{7,8},{8,9},{9,10},{10,1... | collective-permute-start | bytes 663560 | tf_op jit(solution)/shard_map/ppermute | solution.py:259
  64.4 1.9 %collective-permute-start.1 = (f32[3,24,768]{2,1,0:T(8,128)S(1)}, f32[3,24,768]{2,1,0:T(8,128)S(1)}, u32[]{:S(2)}, u32[]{:S(2)}) collective-permute-start(f32[3,24,768]{2,1,0:T(8,128)S(1)} %get-tuple-element.10), channel_id=1, source_target_pairs={{1,0},{2,1},{3,2},{4,3},{5,4},{6,5},{7,6},{8,7},{9,8},{10,9},{11,1... | collective-permute-start | bytes 663560 | tf_op jit(solution)/shard_map/ppermute | solution.py:260
  66.3 1.1 %collective-permute-done.low_ref = f32[3,24,768]{2,1,0:T(8,128)S(1)} collective-permute-done((f32[3,24,768]{2,1,0:T(8,128)S(1)}, f32[3,24,768]{2,1,0:T(8,128)S(1)}, u32[]{:S(2)}, u32[]{:S(2)}) %collective-permute-start) | collective-permute-done | bytes 221216 | tf_op jit(solution)/shard_map/ppermute | solution.py:259
  67.4 11.4 %collective-permute-done.1.high_ref = f32[3,24,768]{2,1,0:T(8,128)S(1)} collective-permute-done((f32[3,24,768]{2,1,0:T(8,128)S(1)}, f32[3,24,768]{2,1,0:T(8,128)S(1)}, u32[]{:S(2)}, u32[]{:S(2)}) %collective-permute-start.1) | collective-permute-done | bytes 221216 | tf_op jit(solution)/shard_map/ppermute | solution.py:260
  78.9 0.8 shard_map.31
Async XLA Ops:
  0.0 0.9 %copy-start.1 = (f32[3,64,8,16]{1,3,2,0:T(8,128)S(1)}, f32[3,64,8,16]{1,3,2,0:T(8,128)}, u32[]{:S(2)}) copy-start(f32[3,64,8,16]{1,3,2,0:T(8,128)} %param.3) | copy-start | bytes 294916
  0.9 15.5 %copy-start = (f32[4,24,768]{2,1,0:T(8,128)S(1)}, f32[4,24,768]{2,1,0:T(8,128)}, u32[]{:S(2)}) copy-start(f32[4,24,768]{2,1,0:T(8,128)} %s_ref.1) | copy-start | bytes 884740
  55.9 11.5 %collective-permute-start = (f32[3,24,768]{2,1,0:T(8,128)S(1)}, f32[3,24,768]{2,1,0:T(8,128)S(1)}, u32[]{:S(2)}, u32[]{:S(2)}) collective-permute-start(f32[3,24,768]{2,1,0:T(8,128)S(1)} %get-tuple-element.9), channel_id=1, source_target_pairs={{0,1},{1,2},{2,3},{3,4},{4,5},{5,6},{6,7},{7,8},{8,9},{9,10},{10,1... | collective-permute-start | bytes 663560 | tf_op jit(solution)/shard_map/ppermute | solution.py:259
  64.4 14.5 %collective-permute-start.1 = (f32[3,24,768]{2,1,0:T(8,128)S(1)}, f32[3,24,768]{2,1,0:T(8,128)S(1)}, u32[]{:S(2)}, u32[]{:S(2)}) collective-permute-start(f32[3,24,768]{2,1,0:T(8,128)S(1)} %get-tuple-element.10), channel_id=1, source_target_pairs={{1,0},{2,1},{3,2},{4,3},{5,4},{6,5},{7,6},{8,7},{9,8},{10,9},{11,1... | collective-permute-start | bytes 663560 | tf_op jit(solution)/shard_map/ppermute | solution.py:260

commit v3 on v2

v3 whole, which is shorter than its diff:
```python
import jax
import jax.numpy as jnp
from jax import lax
from jax.experimental import pallas as pl
from jax.experimental.pallas import tpu as pltpu
from jax.sharding import PartitionSpec as P


F32 = jnp.float32
BF16 = jnp.bfloat16


def iota(shape, dim):
    return lax.broadcasted_iota(jnp.int32, shape, dim)


def remesh_terms(u, before, after, q):
    up = u >= 0.0
    size = jnp.abs(u)
    a = size - (0.5 * size) * (size - jnp.where(up, after, -before))
    b = a - 0.5
    s = b * b
    e1 = (-1.0 / 16.0 * s + 13.0 / 32.0) * s - 25.0 / 256.0
    e2 = (1.0 / 48.0 * s - 5.0 / 96.0) * s + 3.0 / 256.0
    e0 = 0.5 - e1 - e2
    o0 = ((-25.0 / 12.0 * s + 19.0 / 8.0) * s - 281.0 / 192.0) * b
    o1 = ((25.0 / 24.0 * s - 53.0 / 48.0) * s + 27.0 / 128.0) * b
    o2 = ((-5.0 / 24.0 * s + 3.0 / 16.0) * s - 13.0 / 384.0) * b
    at0 = q * (e0 + o0)
    near1, far1 = q * (e0 - o0), q * (e1 + o1)
    near2, far2 = q * (e1 - o1), q * (e2 + o2)
    near3 = q * (e2 - o2)
    zero = jnp.zeros_like(q)
    return {
        0: at0,
        1: jnp.where(up, near1, far1),
        -1: jnp.where(up, far1, near1),
        2: jnp.where(up, near2, far2),
        -2: jnp.where(up, far2, near2),
        3: jnp.where(up, near3, zero),
        -3: jnp.where(up, zero, near3),
    }


def roll(x, shift, axis):
    n = x.shape[axis]
    shift = shift % n
    return x if shift == 0 else pltpu.roll(x, shift, axis)


def sweep_ring(q, u, axis):
    terms = remesh_terms(u, roll(u, 1, axis), roll(u, -1, axis), q)
    total = terms[0]
    for m in (1, -1, 2, -2, 3, -3):
        total = total + roll(terms[m], m, axis)
    return total


def swap_blocks(x):
    row = iota((8, 128), 0)
    block = iota((8, 128), 1) >> 4
    for bit in (1, 2, 4):
        low = (row & bit) == 0
        first = (block & bit) == 0
        upward = roll(roll(x, -bit, 0), 16 * bit, 1)
        downward = roll(roll(x, bit, 0), -16 * bit, 1)
        x = jnp.where(low == first, x, jnp.where(low, upward, downward))
    return x


def pack_velocity(v_ref, out_ref):
    lane = iota((8, 128), 1)
    tiles = []
    for c in range(3):
        block = v_ref[c].reshape(128, 64)
        block = jnp.concatenate([block, jnp.zeros((128, 64), F32)], axis=1).T
        tiles.append([swap_blocks(block[8 * n : 8 * n + 8]) for n in range(8)])
    zero = jnp.zeros((8, 128), F32)
    for k in range(16):
        n, odd = divmod(k, 2)
        if odd == 0:
            out_ref[k, 0:8, :] = jnp.where(lane < 64, tiles[0][n], roll(tiles[1][n], 64, 1))
            before = tiles[2][n - 1] if n > 0 else zero
            planes = jnp.where(lane < 16, roll(before, 16, 1), roll(tiles[2][n], 16, 1))
        else:
            out_ref[k, 0:8, :] = jnp.where(lane < 64, roll(tiles[0][n], -64, 1), tiles[1][n])
            after = tiles[2][n + 1] if n < 7 else zero
            planes = jnp.where(lane < 80, roll(tiles[2][n], -48, 1), roll(after, 80, 1))
        out_ref[k, 8:16, :] = jnp.where(lane < 96, planes, zero)


def odd_device():
    return lax.axis_index("gz") & 1


def pack_scalar(s_ref, out_ref, t_ref):
    flip = odd_device() * 3
    for v in range(6):
        part = slice(128 * v, 128 * v + 128)
        block = jnp.concatenate([s_ref[p ^ flip, :, part] for p in range(4)] + [jnp.zeros((32, 128), F32)], axis=0)
        t_ref[part, :] = block.T
    lane = iota((8, 128), 1)
    row = iota((8, 128), 0)
    for i in range(32):
        left = t_ref[(24 * i - 8) % 768 : (24 * i - 8) % 768 + 8, :]
        right = t_ref[(24 * i + 24) % 768 : (24 * i + 24) % 768 + 8, :]
        halo = jnp.where(row < 4, right, left)
        for t in range(3):
            tile = t_ref[24 * i + 8 * t : 24 * i + 8 * t + 8, :]
            out_ref[i, 8 * t : 8 * t + 8, :] = jnp.where(lane < 96, tile, roll(halo, 96 - 32 * t, 1))


def add_velocity(old_ref, r_ref, out_ref):
    lane = iota((8, 128), 1)
    row = iota((8, 128), 0)
    col = lane & 15
    slot = lane >> 4
    for i in range(32):
        k = i // 2
        here, depth = r_ref[k, 0:8, :], r_ref[k, 8:16, :]
        if i % 2 == 0:
            other = r_ref[(k - 1) % 16, 0:8, :]
            wide = jnp.where(col == 0, roll(other, -15, 1), roll(here, 1, 1))
            near = here
        else:
            other = r_ref[(k + 1) % 16, 0:8, :]
            wide = jnp.where(col < 9, roll(here, -7, 1), roll(other, 9, 1))
            near = jnp.where(col < 8, roll(here, -8, 1), roll(other, 8, 1))
            depth = jnp.where(col < 8, roll(depth, -8, 1), roll(r_ref[(k + 1) % 16, 8:16, :], 8, 1))
        tile = jnp.where(slot < 4, wide, near)
        tile = jnp.where((slot >= 4) & (col >= 9), roll(depth, 73, 1), tile)
        tile = jnp.where((slot < 2) & (col >= 11), roll(depth, -53, 1), tile)
        tile = jnp.where(((slot >> 1) == 1) & (col >= 11), roll(depth, -26, 1), tile)
        out_ref[i, 24:32, :] = tile
        rest = jnp.where((slot < 4) & ((col == 7) | (col == 8)), depth, 0.0)
        rest = pltpu.roll(rest, 0, 1, stride=2, stride_axis=0)
        stash = jnp.broadcast_to(jnp.sum(rest, axis=0, keepdims=True), (8, 128))
        for t in range(3):
            rows = slice(8 * t, 8 * t + 8)
            out_ref[i, rows, :] = jnp.where((row == 3) & (lane >= 96), roll(stash, 96 - 32 * t, 1), old_ref[i, rows, :])


def hat_rows(rows, slot, ring):
    e = iota((rows, 128), 0)
    if ring:
        e = jnp.where(e > 28, e - 32, e) + 3
    lane = iota((rows, 128), 1)
    away = jnp.abs(e - 3 * (lane & 15))
    return jnp.where((lane >> 4) == slot, jnp.maximum(3 - away, 0), 0)


def weights(y_ref, near_ref, near_z_ref, far_ref, far_z_ref):
    odd = odd_device()
    for v in range(6):
        c = iota((256, 128), 0)
        f = iota((256, 128), 1) + 128 * v
        away = jnp.abs(f - 3 * c)
        away = jnp.minimum(away, 768 - away)
        y_ref[:, 128 * v : 128 * v + 128] = jnp.maximum(3 - away, 0).astype(F32).astype(BF16)

    def both(rows):
        return jnp.concatenate(rows, axis=0).astype(F32).astype(BF16)

    sign = 1 - 2 * odd
    for planes, speeds, xy_ref, z_ref in (((0, 1, 2), range(5), near_ref, near_z_ref), ((3,), (3, 4, 5), far_ref, far_z_ref)):
        xy = both([hat_rows(32, p ^ (3 * odd), True) for p in planes] + [hat_rows(24, 4 + (p ^ (3 * odd)), False) for p in planes])
        z = both([hat_rows(24, jnp.where(odd == 1, 5 - p, p), False) * sign for p in speeds])
        xy_ref[:, 0:128] = xy
        xy_ref[:, 128:256] = xy
        z_ref[:, 0:128] = z
        z_ref[:, 128:256] = z


def two_pieces(x):
    hi = x.astype(BF16)
    return jnp.concatenate([hi, (x - hi.astype(F32)).astype(BF16)], axis=0)


def unpack(s_ref, f_ref, c_ref, planes):
    lane = iota((8, 128), 1)
    row = iota((8, 128), 0)
    col = lane & 15
    slot = lane >> 4
    for i in range(32):
        tiles = [s_ref[i, 8 * t : 8 * t + 8, :] for t in range(3)]
        halo = jnp.where(lane < 32, roll(tiles[0], -96, 1), jnp.where(lane < 64, roll(tiles[1], -64, 1), roll(tiles[2], -32, 1)))
        v, at = divmod(24 * i, 128)
        here = min(24, 128 - at)
        for t, tile in enumerate(tiles + [halo]):
            rows = slice(8 * t, 8 * t + 8)
            for n, p in enumerate(planes):
                moved = roll(tile, at - 24 * p, 1)
                f_ref[n, rows, 128 * v + at : 128 * v + at + here] = moved[:, at : at + here]
                if here < 24:
                    f_ref[n, rows, 128 * v + 128 : 128 * v + 128 + 24 - here] = moved[:, : 24 - here]
        packed = s_ref[i, 24:32, :]
        rest = jnp.broadcast_to(halo[3:4, :], (8, 128))
        for bit in (1, 2, 4):
            rest = jnp.where((row & bit) == 0, rest, roll(rest, -2 * bit, 1))
        depth = jnp.where(slot >= 4, jnp.where(col < 5, roll(packed, 53, 1), roll(packed, 26, 1)), jnp.where(col < 7, roll(packed, -73, 1), rest))
        c_ref[0, 8 * i : 8 * i + 8, :] = packed * (1.0 / 9.0)
        c_ref[1, 8 * i : 8 * i + 8, :] = depth * (1.0 / 9.0)


def refine(coarse, y_ref, hats_ref):
    both = jnp.dot(two_pieces(coarse.T), y_ref[...], preferred_element_type=F32)
    return jnp.dot(hats_ref[...], two_pieces(both[:128] + both[128:]), preferred_element_type=F32)


def plane_sweeps(f_ref, u_ref, x_ref, q_ref, count):
    def along_x(v, carry):
        part = pl.ds(pl.multiple_of(128 * v, 128), 128)
        for p in range(count):
            x_ref[p, :, part] = sweep_ring(f_ref[p, :, part], u_ref[32 * p : 32 * p + 32, part], 0)[:24]
        return carry

    lax.fori_loop(0, 6, along_x, 0)

    def along_y(t, carry):
        for p in range(count):
            rows = pl.ds(pl.multiple_of(8 * t, 8), 8)
            speed = u_ref[pl.ds(pl.multiple_of(32 * count + 24 * p + 8 * t, 8), 8), :]
            q_ref[p, rows, :] = sweep_ring(x_ref[p, rows, :], speed, 1)
        return carry

    lax.fori_loop(0, 3, along_y, 0)


def near_planes(s_ref, y_ref, hats_ref, hats_z_ref, outer_ref, own_ref, inner_ref, f_ref, c_ref, u_ref, w_ref, x_ref, q_ref):
    unpack(s_ref, f_ref, c_ref, (0, 1, 2))
    u_ref[...] = refine(c_ref[0], y_ref, hats_ref)
    w_ref[...] = refine(c_ref[1], y_ref, hats_z_ref)
    plane_sweeps(f_ref, u_ref, x_ref, q_ref, 3)

    def along_z(v, carry):
        part = pl.ds(pl.multiple_of(128 * v, 128), 128)
        for t in range(3):
            rows = slice(8 * t, 8 * t + 8)
            speeds = [w_ref[24 * p + 8 * t : 24 * p + 8 * t + 8, part] for p in range(5)]
            total = {}
            for p in range(3):
                terms = remesh_terms(speeds[p + 1], speeds[p], speeds[p + 2], q_ref[p, rows, part])
                for m, term in terms.items():
                    total[p + m] = total[p + m] + term if p + m in total else term
            for n in range(3):
                outer_ref[n, rows, part] = total[-1 - n]
            for n in range(4):
                own_ref[n, rows, part] = total[n]
            for n in range(2):
                inner_ref[n, rows, part] = total[4 + n]
        return carry

    lax.fori_loop(0, 6, along_z, 0)


def far_plane(s_ref, y_ref, hats_ref, hats_z_ref, some_ref, rest_ref, own_ref, inner_ref, f_ref, c_ref, u_ref, w_ref, x_ref, q_ref):
    unpack(s_ref, f_ref, c_ref, (3,))
    u_ref[...] = refine(c_ref[0], y_ref, hats_ref)
    w_ref[...] = refine(c_ref[1], y_ref, hats_z_ref)
    plane_sweeps(f_ref, u_ref, x_ref, q_ref, 1)

    def along_z(v, carry):
        part = pl.ds(pl.multiple_of(128 * v, 128), 128)
        for t in range(3):
            rows = slice(8 * t, 8 * t + 8)
            before, speed, after = [w_ref[24 * p + 8 * t : 24 * p + 8 * t + 8, part] for p in range(3)]
            terms = remesh_terms(speed, before, after, q_ref[0, rows, part])
            for n in range(4):
                own_ref[n, rows, part] = some_ref[n, rows, part] + terms[n - 3]
            for n in range(2):
                inner_ref[n, rows, part] = rest_ref[n, rows, part] + terms[1 + n]
            inner_ref[2, rows, part] = terms[3]
        return carry

    lax.fori_loop(0, 6, along_z, 0)


def join(own_ref, outer_ref, inner_ref, out_ref):
    flip = odd_device() * 3
    out_ref[0 ^ flip] = own_ref[0] + outer_ref[0]
    out_ref[1 ^ flip] = own_ref[1] + outer_ref[1] + inner_ref[2]
    out_ref[2 ^ flip] = own_ref[2] + outer_ref[2] + inner_ref[1]
    out_ref[3 ^ flip] = own_ref[3] + inner_ref[0]


def kernel(body, *shapes, scratch=(), alias=None, flops=1e7):
    outs = tuple(jax.ShapeDtypeStruct(*(s if isinstance(s[0], tuple) else (s, F32))) for s in shapes)
    return pl.pallas_call(
        body,
        out_shape=outs if len(outs) > 1 else outs[0],
        scratch_shapes=[pltpu.VMEM(s, F32) for s in scratch],
        input_output_aliases=alias or {},
        cost_estimate=pl.CostEstimate(flops=int(flops), transcendentals=0, bytes_accessed=1 << 20),
        compiler_params=pltpu.CompilerParams(vmem_limit_bytes=16 * 1024 * 1024),
    )


def exchange(x, axis):
    return lax.all_to_all(x, axis, split_axis=0, concat_axis=0, tiled=False)


def sweep_scratch(count, speeds):
    return [(count, 32, 768), (2, 256, 128), (56 * count, 768), (24 * speeds, 768), (count, 24, 768), (count, 24, 768)]


def steps(scalar, velocity):
    planes = exchange(kernel(pack_velocity, (16, 16, 128))(jnp.transpose(velocity, (0, 2, 3, 1))), "gz")
    chunks = kernel(pack_scalar, (32, 32, 128), scratch=[(768, 128)])(scalar)
    tables = ((256, 768), (168, 256), (120, 256), (56, 256), (72, 256))
    y_weights, near, near_z, far, far_z = kernel(weights, *((s, BF16) for s in tables))()
    chunks = exchange(kernel(add_velocity, (32, 32, 128), alias={0: 0})(chunks, planes), "gy")
    outer, own, inner = kernel(near_planes, (3, 24, 768), (4, 24, 768), (2, 24, 768), scratch=sweep_scratch(3, 5))(chunks, y_weights, near, near_z)
    count = lax.axis_size("gz")
    pairs = [(k, k + 1) for k in range(1, count - 1, 2)]
    outer = lax.ppermute(outer, "gz", pairs + [(b, a) for a, b in pairs])
    own, inner = kernel(far_plane, (4, 24, 768), (3, 24, 768), scratch=sweep_scratch(1, 3), flops=1e9)(chunks, y_weights, far, far_z, own, inner)
    pairs = [(k, k + 1) for k in range(0, count, 2)]
    inner = lax.ppermute(inner, "gz", pairs + [(b, a) for a, b in pairs])
    return kernel(join, (4, 24, 768))(own, outer, inner)


def solution(mesh):
    in_specs = (P("gz", "gy", None), P(None, None, "gy", "gz"))
    out_specs = P("gz", "gy", None)
    return jax.shard_map(steps, mesh=mesh, in_specs=in_specs, out_specs=out_specs, check_vma=False)
```

time: 79.9 us -> 82.3 us (1.030)
  the two profiles are of different devices: /device:TPU:57 before, /device:TPU:17 now
where the time goes in v3:
time: 82.3 us; the launch traced here: 81.9 us
  waiting for transfers between devices  39.4 us (48%)
  starting transfers between devices  28.5 us (35%)
  Pallas kernels  13 us (16%)
  local copies, waits for them, and re-layouts  0.93 us (1%)
    all_to_all x2, waiting for transfers between devices, exchange(): return lax.all_to_all(x, axis, split_axis=0, concat_axis=0, tiled=False)  24 us
    all_to_all x2, starting transfers between devices, exchange(): return lax.all_to_all(x, axis, split_axis=0, concat_axis=0, tiled=False)  22 us
    ppermute x1, waiting for transfers between devices, steps(): outer = lax.ppermute(outer, 'gz', pairs + [(b, a) for a, b in pairs])  15.5 us
    pallas_call x1, Pallas kernels, steps(): kernel(add_velocity, (32, 32, 128), alias={0: 0})(chunks, planes)  3.93 us
    ppermute x1, starting transfers between devices, steps(): inner = lax.ppermute(inner, 'gz', pairs + [(b, a) for a, b in pairs])  3.83 us
    pallas_call x1, Pallas kernels, steps(): kernel(near_planes, (3, 24, 768), (4, 24, 768), (2, 24, 768), scratch=swe...  3.55 us
    ppermute x1, starting transfers between devices, steps(): outer = lax.ppermute(outer, 'gz', pairs + [(b, a) for a, b in pairs])  2.67 us
    pallas_call x1, Pallas kernels, steps(): kernel(far_plane, (4, 24, 768), (3, 24, 768), scratch=sweep_scratch(1, 3)...  2.11 us
  transfers between devices with their start and end apart: 4, of which 3 were waited for; matrix products, arithmetic and copies ran while one was open for 0% of the time, Pallas kernels for 2%

profile of v3, /device:TPU:17, one launch (start us, length us, event | category | flops | bytes accessed | tf_op | source)
XLA Modules:
  0.0 81.9 jit_solution(8792321858978941606)
XLA Ops:
  0.0 0.0 copy-start.1
  0.0 0.9 %copy-done.1 = f32[3,64,8,16]{1,3,2,0:T(8,128)S(1)} copy-done((f32[3,64,8,16]{1,3,2,0:T(8,128)S(1)}, f32[3,64,8,16]{1,3,2,0:T(8,128)}, u32[]{:S(2)}) %copy-start.1) | copy-done | bytes 98328
  0.9 0.0 copy-start
  0.9 1.1 %shard_map.29 = f32[16,16,128]{2,1,0:T(8,128)} custom-call(f32[3,8,16,64]{3,2,1,0:T(8,128)S(1)} %bitcast.1), custom_call_target="tpu_custom_call" | custom-call | flops 10000000 | bytes 1048576 | tf_op jit(solution)/shard_map/pallas_call | solution.py:307
  2.0 8.4 %all-to-all-start = ((f32[16,16,128]{2,1,0:T(8,128)}), f32[16,16,128]{2,1,0:T(8,128)S(1)}, u32[]{:S(2)}, u32[]{:S(2)}) async-start(f32[16,16,128]{2,1,0:T(8,128)} %shard_map.29), calls=%async_computation | async-start | bytes 262144 | tf_op jit(solution)/shard_map/all_to_all | solution.py:299
  10.5 0.0 copy-done
  10.5 1.1 %shard_map.28.old_ref = f32[32,32,128]{2,1,0:T(8,128)} custom-call(f32[4,24,768]{2,1,0:T(8,128)S(1)} %copy-done), custom_call_target="tpu_custom_call" | custom-call | flops 10000000 | bytes 1048576 | tf_op jit(solution)/shard_map/pallas_call | solution.py:308
  11.6 8.9 %all-to-all-done.r_ref = f32[16,16,128]{2,1,0:T(8,128)S(1)} async-done(((f32[16,16,128]{2,1,0:T(8,128)}), f32[16,16,128]{2,1,0:T(8,128)S(1)}, u32[]{:S(2)}, u32[]{:S(2)}) %all-to-all-start) | async-done | bytes 131104 | tf_op jit(solution)/shard_map/all_to_all | solution.py:299
  20.5 3.9 %shard_map.30 = f32[32,32,128]{2,1,0:T(8,128)} custom-call(f32[32,32,128]{2,1,0:T(8,128)} %shard_map.28.old_ref, f32[16,16,128]{2,1,0:T(8,128)S(1)} %all-to-all-done.r_ref), custom_call_target="tpu_custom_call", output_to_operand_aliasing={{}: (0, {})} | custom-call | flops 10000000 | bytes 1048576 | tf_op jit(solution)/shard_map/pallas_call | solution.py:311
  24.5 13.6 %all-to-all-start.1 = ((f32[32,32,128]{2,1,0:T(8,128)}), f32[32,32,128]{2,1,0:T(8,128)S(1)}, u32[]{:S(2)}, u32[]{:S(2)}) async-start(f32[32,32,128]{2,1,0:T(8,128)} %shard_map.30), calls=%async_computation.1 | async-start | bytes 1048576 | tf_op jit(solution)/shard_map/all_to_all | solution.py:299
  38.0 0.3 shard_map.31
  38.4 15.1 %all-to-all-done.1.s_ref = f32[32,32,128]{2,1,0:T(8,128)S(1)} async-done(((f32[32,32,128]{2,1,0:T(8,128)}), f32[32,32,128]{2,1,0:T(8,128)S(1)}, u32[]{:S(2)}, u32[]{:S(2)}) %all-to-all-start.1) | async-done | bytes 524320 | tf_op jit(solution)/shard_map/all_to_all | solution.py:299
  53.5 3.6 %shard_map.32 = (f32[3,24,768]{2,1,0:T(8,128)S(1)}, f32[4,24,768]{2,1,0:T(8,128)S(1)}, f32[2,24,768]{2,1,0:T(8,128)S(1)}) custom-call(f32[32,32,128]{2,1,0:T(8,128)S(1)} %all-to-all-done.1.s_ref, bf16[256,768]{1,0:T(8,128)(2,1)S(1)} %get-tuple-element.15.y_ref, bf16[168,256]{1,0:T(8,128)(2,1)S(1)} %get-tuple-element.18.hats_ref, ...), custom_call_target="tpu_custom_call" | custom-call | flops 10000000 | bytes 1048576 | tf_op jit(solution)/shard_map/pallas_call | solution.py:312
  57.0 2.1 %shard_map.33 = (f32[4,24,768]{2,1,0:T(8,128)S(1)}, f32[3,24,768]{2,1,0:T(8,128)S(1)}) custom-call(f32[32,32,128]{2,1,0:T(8,128)S(1)} %all-to-all-done.1.s_ref, bf16[256,768]{1,0:T(8,128)(2,1)S(1)} %get-tuple-element.15.y_ref, bf16[56,256]{1,0:T(8,128)(2,1)S(1)} %get-tuple-element.16.hats_ref, bf16[72,256]{1,0:T(8,128)(2,1)S(1)} %get-tuple-element.17.hats_z_ref, ...), custom_call_target="tpu_custom_call" | custom-call | flops 1000000000 | bytes 1048576 | tf_op jit(solution)/shard_map/pallas_call | solution.py:316
  59.2 3.8 %collective-permute-start.1 = (f32[3,24,768]{2,1,0:T(8,128)S(1)}, f32[3,24,768]{2,1,0:T(8,128)S(1)}, u32[]{:S(2)}, u32[]{:S(2)}) collective-permute-start(f32[3,24,768]{2,1,0:T(8,128)S(1)} %get-tuple-element.24), channel_id=1, source_target_pairs={{0,1},{2,3},{4,5},{6,7},{8,9},{10,11},{12,13},{14,15},{1,0},{3,2},... | collective-permute-start | bytes 663560 | tf_op jit(solution)/shard_map/ppermute | solution.py:318
  63.0 2.7 %collective-permute-start = (f32[3,24,768]{2,1,0:T(8,128)S(1)}, f32[3,24,768]{2,1,0:T(8,128)S(1)}, u32[]{:S(2)}, u32[]{:S(2)}) collective-permute-start(f32[3,24,768]{2,1,0:T(8,128)S(1)} %get-tuple-element.23), channel_id=1, source_target_pairs={{1,2},{3,4},{5,6},{7,8},{9,10},{11,12},{13,14},{2,1},{4,3},{6,5},{... | collective-permute-start | bytes 663560 | tf_op jit(solution)/shard_map/ppermute | solution.py:315
  65.7 0.0 collective-permute-done.1.inner_ref
  65.7 15.5 %collective-permute-done.outer_ref = f32[3,24,768]{2,1,0:T(8,128)S(1)} collective-permute-done((f32[3,24,768]{2,1,0:T(8,128)S(1)}, f32[3,24,768]{2,1,0:T(8,128)S(1)}, u32[]{:S(2)}, u32[]{:S(2)}) %collective-permute-start) | collective-permute-done | bytes 221216 | tf_op jit(solution)/shard_map/ppermute | solution.py:315
  81.1 0.8 shard_map.34
Async XLA Ops:
  0.0 0.9 %copy-start.1 = (f32[3,64,8,16]{1,3,2,0:T(8,128)S(1)}, f32[3,64,8,16]{1,3,2,0:T(8,128)}, u32[]{:S(2)}) copy-start(f32[3,64,8,16]{1,3,2,0:T(8,128)} %param.3) | copy-start | bytes 294916
  0.9 9.6 %copy-start = (f32[4,24,768]{2,1,0:T(8,128)S(1)}, f32[4,24,768]{2,1,0:T(8,128)}, u32[]{:S(2)}) copy-start(f32[4,24,768]{2,1,0:T(8,128)} %s_ref.1) | copy-start | bytes 884740
  2.0 18.5 %all-to-all-start = ((f32[16,16,128]{2,1,0:T(8,128)}), f32[16,16,128]{2,1,0:T(8,128)S(1)}, u32[]{:S(2)}, u32[]{:S(2)}) async-start(f32[16,16,128]{2,1,0:T(8,128)} %shard_map.29), calls=%async_computation | async-start | bytes 262144 | tf_op jit(solution)/shard_map/all_to_all | solution.py:299
  24.5 29.0 %all-to-all-start.1 = ((f32[32,32,128]{2,1,0:T(8,128)}), f32[32,32,128]{2,1,0:T(8,128)S(1)}, u32[]{:S(2)}, u32[]{:S(2)}) async-start(f32[32,32,128]{2,1,0:T(8,128)} %shard_map.30), calls=%async_computation.1 | async-start | bytes 1048576 | tf_op jit(solution)/shard_map/all_to_all | solution.py:299
  59.2 6.5 %collective-permute-start.1 = (f32[3,24,768]{2,1,0:T(8,128)S(1)}, f32[3,24,768]{2,1,0:T(8,128)S(1)}, u32[]{:S(2)}, u32[]{:S(2)}) collective-permute-start(f32[3,24,768]{2,1,0:T(8,128)S(1)} %get-tuple-element.24), channel_id=1, source_target_pairs={{0,1},{2,3},{4,5},{6,7},{8,9},{10,11},{12,13},{14,15},{1,0},{3,2},... | collective-permute-start | bytes 663560 | tf_op jit(solution)/shard_map/ppermute | solution.py:318
  63.0 18.1 %collective-permute-start = (f32[3,24,768]{2,1,0:T(8,128)S(1)}, f32[3,24,768]{2,1,0:T(8,128)S(1)}, u32[]{:S(2)}, u32[]{:S(2)}) collective-permute-start(f32[3,24,768]{2,1,0:T(8,128)S(1)} %get-tuple-element.23), channel_id=1, source_target_pairs={{1,2},{3,4},{5,6},{7,8},{9,10},{11,12},{13,14},{2,1},{4,3},{6,5},{... | collective-permute-start | bytes 663560 | tf_op jit(solution)/shard_map/ppermute | solution.py:315

commit v4 on v3

--- a/solution.py
+++ b/solution.py
@@ -133,8 +133,9 @@
         tile = jnp.where(((slot >> 1) == 1) & (col >= 11), roll(depth, -26, 1), tile)
         out_ref[i, 24:32, :] = tile
         rest = jnp.where((slot < 4) & ((col == 7) | (col == 8)), depth, 0.0)
-        rest = pltpu.roll(rest, 0, 1, stride=2, stride_axis=0)
-        stash = jnp.broadcast_to(jnp.sum(rest, axis=0, keepdims=True), (8, 128))
+        for bit in (4, 2, 1):
+            rest = rest + roll(roll(rest, -bit, 0), 2 * bit, 1)
+        stash = roll(rest, 3, 0)
         for t in range(3):
             rows = slice(8 * t, 8 * t + 8)
             out_ref[i, rows, :] = jnp.where((row == 3) & (lane >= 96), roll(stash, 96 - 32 * t, 1), old_ref[i, rows, :])
@@ -169,6 +170,12 @@
         xy_ref[:, 128:256] = xy
         z_ref[:, 0:128] = z
         z_ref[:, 128:256] = z
+
+
+def prepare(v_ref, s_ref, planes_ref, out_ref, y_ref, near_ref, near_z_ref, far_ref, far_z_ref, t_ref):
+    pack_velocity(v_ref, planes_ref)
+    pack_scalar(s_ref, out_ref, t_ref)
+    weights(y_ref, near_ref, near_z_ref, far_ref, far_z_ref)
 
 
 def two_pieces(x):
@@ -304,10 +311,10 @@
 
 
 def steps(scalar, velocity):
-    planes = exchange(kernel(pack_velocity, (16, 16, 128))(jnp.transpose(velocity, (0, 2, 3, 1))), "gz")
-    chunks = kernel(pack_scalar, (32, 32, 128), scratch=[(768, 128)])(scalar)
-    tables = ((256, 768), (168, 256), (120, 256), (56, 256), (72, 256))
-    y_weights, near, near_z, far, far_z = kernel(weights, *((s, BF16) for s in tables))()
+    tables = [(t, BF16) for t in ((256, 768), (168, 256), (120, 256), (56, 256), (72, 256))]
+    coarse = jnp.transpose(velocity, (0, 2, 3, 1))
+    planes, chunks, y_weights, near, near_z, far, far_z = kernel(prepare, (16, 16, 128), (32, 32, 128), *tables, scratch=[(768, 128)])(coarse, scalar)
+    planes = exchange(planes, "gz")
     chunks = exchange(kernel(add_velocity, (32, 32, 128), alias={0: 0})(chunks, planes), "gy")
     outer, own, inner = kernel(near_planes, (3, 24, 768), (4, 24, 768), (2, 24, 768), scratch=sweep_scratch(3, 5))(chunks, y_weights, near, near_z)
     count = lax.axis_size("gz")

time: 82.3 us -> 82 us (level)
  blocking collectives: 0 us -> 47.1 us
  waiting for transfers between devices: 39.4 us -> 15.5 us
  starting transfers between devices: 28.5 us -> 6.5 us
  Pallas kernels: 13 us -> 10.8 us
  local copies, waits for them, and re-layouts: 0.93 us -> 1.89 us
    all_to_all x0 -> x2, blocking collectives: none -> 47.1 us  [exchange(): return lax.all_to_all(x, axis, split_axis=0, concat_axis=0, tiled=False)]
    all_to_all x2 -> x0, waiting for transfers between devices: 24 us -> none  [exchange(): return lax.all_to_all(x, axis, split_axis=0, concat_axis=0, tiled=False)]
    all_to_all x2 -> x0, starting transfers between devices: 22 us -> none  [exchange(): return lax.all_to_all(x, axis, split_axis=0, concat_axis=0, tiled=False)]
    pallas_call x1, Pallas kernels: 3.93 us -> 2.7 us  [steps(): kernel(add_velocity, (32, 32, 128), alias={0: 0})(chunks, planes)]
    unnamed x4, local copies, waits for them, and re-layouts: 0.93 us -> 1.89 us
    pallas_call x3 -> x1, Pallas kernels: 2.59 us -> 1.66 us  [steps(): kernel(prepare, (16, 16, 128), (32, 32, 128), *tables, scratch=[(768, 128)])]
  transfers between devices with their start and end apart: 4 -> 2, of which waited for: 3 -> 1; matrix products, arithmetic and copies ran while one was open for 0% -> 0% of each run, Pallas kernels for 2% -> 0%
where the time goes in v4:
time: 82 us; the launch traced here: 81.8 us
  blocking collectives  47.1 us (57%)
  waiting for transfers between devices  15.5 us (19%)
  Pallas kernels  10.8 us (13%)
  starting transfers between devices  6.5 us (8%)
  local copies, waits for them, and re-layouts  1.89 us (2%)
    all_to_all x2, blocking collectives, exchange(): return lax.all_to_all(x, axis, split_axis=0, concat_axis=0, tiled=False)  47.1 us
    ppermute x1, waiting for transfers between devices, steps(): outer = lax.ppermute(outer, 'gz', pairs + [(b, a) for a, b in pairs])  15.5 us
    ppermute x1, starting transfers between devices, steps(): inner = lax.ppermute(inner, 'gz', pairs + [(b, a) for a, b in pairs])  3.83 us
    pallas_call x1, Pallas kernels, steps(): kernel(near_planes, (3, 24, 768), (4, 24, 768), (2, 24, 768), scratch=swe...  3.56 us
    pallas_call x1, Pallas kernels, steps(): kernel(add_velocity, (32, 32, 128), alias={0: 0})(chunks, planes)  2.7 us
    ppermute x1, starting transfers between devices, steps(): outer = lax.ppermute(outer, 'gz', pairs + [(b, a) for a, b in pairs])  2.67 us
    pallas_call x1, Pallas kernels, steps(): kernel(far_plane, (4, 24, 768), (3, 24, 768), scratch=sweep_scratch(1, 3)...  2.12 us
    unnamed x4, local copies, waits for them, and re-layouts  1.89 us
  transfers between devices with their start and end apart: 2, of which 1 were waited for; matrix products, arithmetic and copies ran while one was open for 0% of the time, Pallas kernels for 0%

profile of v4, /device:TPU:17, one launch (start us, length us, event | category | flops | bytes accessed | tf_op | source)
XLA Modules:
  0.0 81.8 jit_solution(2767089765983744704)
XLA Ops:
  0.0 0.0 copy-start
  0.0 1.0 %copy-done = f32[4,24,768]{2,1,0:T(8,128)S(1)} copy-done((f32[4,24,768]{2,1,0:T(8,128)S(1)}, f32[4,24,768]{2,1,0:T(8,128)}, u32[]{:S(2)}) %copy-start) | copy-done | bytes 294936
  1.0 0.0 copy-start.1
  1.0 0.9 %copy-done.1 = f32[3,64,8,16]{1,3,2,0:T(8,128)S(1)} copy-done((f32[3,64,8,16]{1,3,2,0:T(8,128)S(1)}, f32[3,64,8,16]{1,3,2,0:T(8,128)}, u32[]{:S(2)}) %copy-start.1) | copy-done | bytes 98328
  1.9 1.7 %shard_map.28 = (f32[16,16,128]{2,1,0:T(8,128)S(1)}, f32[32,32,128]{2,1,0:T(8,128)S(1)}, bf16[256,768]{1,0:T(8,128)(2,1)S(1)}, bf16[168,256]{1,0:T(8,128)(2,1)S(...) custom-call(f32[3,8,16,64]{3,2,1,0:T(8,128)S(1)} %bitcast.1, ...), custom_call_target="tpu_custom_call" | custom-call | flops 10000000 | bytes 1048576 | tf_op jit(solution)/shard_map/pallas_call | solution.py:316
  3.6 18.3 %all_to_all.10.r_ref = f32[16,16,128]{2,1,0:T(8,128)S(1)} all-to-all(f32[16,16,128]{2,1,0:T(8,128)S(1)} %get-tuple-element.18), channel_id=1, replica_groups=mesh['gy'=32,'gz'=16] {'gz'}, dimensions={0} | all-to-all | bytes 262144 | tf_op jit(solution)/shard_map/all_to_all | solution.py:306
  21.8 2.7 %shard_map.29 = f32[32,32,128]{2,1,0:T(8,128)S(1)} custom-call(f32[32,32,128]{2,1,0:T(8,128)S(1)} %get-tuple-element.17.old_ref, f32[16,16,128]{2,1,0:T(8,128)S(1)} %all_to_all.10.r_ref), custom_call_target="tpu_custom_call", output_to_operand_aliasing={{}: (0, {})} | custom-call | flops 10000000 | bytes 1048576 | tf_op jit(solution)/shard_map/pallas_call | solution.py:318
  24.5 28.8 %all_to_all.11.s_ref = f32[32,32,128]{2,1,0:T(8,128)S(1)} all-to-all(f32[32,32,128]{2,1,0:T(8,128)S(1)} %shard_map.29), channel_id=1, replica_groups=mesh['gy'=32,'gz'=16] {'gy'}, dimensions={0} | all-to-all | bytes 1048576 | tf_op jit(solution)/shard_map/all_to_all | solution.py:306
  53.3 3.6 %shard_map.30 = (f32[3,24,768]{2,1,0:T(8,128)S(1)}, f32[4,24,768]{2,1,0:T(8,128)S(1)}, f32[2,24,768]{2,1,0:T(8,128)S(1)}) custom-call(f32[32,32,128]{2,1,0:T(8,128)S(1)} %all_to_all.11.s_ref, bf16[256,768]{1,0:T(8,128)(2,1)S(1)} %get-tuple-element.19.y_ref, bf16[168,256]{1,0:T(8,128)(2,1)S(1)} %get-tuple-element.22.hats_ref, ...), custom_call_target="tpu_custom_call" | custom-call | flops 10000000 | bytes 1048576 | tf_op jit(solution)/shard_map/pallas_call | solution.py:319
  56.9 2.1 %shard_map.31 = (f32[4,24,768]{2,1,0:T(8,128)S(1)}, f32[3,24,768]{2,1,0:T(8,128)S(1)}) custom-call(f32[32,32,128]{2,1,0:T(8,128)S(1)} %all_to_all.11.s_ref, bf16[256,768]{1,0:T(8,128)(2,1)S(1)} %get-tuple-element.19.y_ref, bf16[56,256]{1,0:T(8,128)(2,1)S(1)} %get-tuple-element.20.hats_ref, bf16[72,256]{1,0:T(8,128)(2,1)S(1)} %get-tuple-element.21.hats_z_ref, ...), custom_call_target="tpu_custom_call" | custom-call | flops 1000000000 | bytes 1048576 | tf_op jit(solution)/shard_map/pallas_call | solution.py:323
  59.0 3.8 %collective-permute-start.1 = (f32[3,24,768]{2,1,0:T(8,128)S(1)}, f32[3,24,768]{2,1,0:T(8,128)S(1)}, u32[]{:S(2)}, u32[]{:S(2)}) collective-permute-start(f32[3,24,768]{2,1,0:T(8,128)S(1)} %get-tuple-element.28), channel_id=1, source_target_pairs={{0,1},{2,3},{4,5},{6,7},{8,9},{10,11},{12,13},{14,15},{1,0},{3,2},... | collective-permute-start | bytes 663560 | tf_op jit(solution)/shard_map/ppermute | solution.py:325
  62.9 2.7 %collective-permute-start = (f32[3,24,768]{2,1,0:T(8,128)S(1)}, f32[3,24,768]{2,1,0:T(8,128)S(1)}, u32[]{:S(2)}, u32[]{:S(2)}) collective-permute-start(f32[3,24,768]{2,1,0:T(8,128)S(1)} %get-tuple-element.27), channel_id=1, source_target_pairs={{1,2},{3,4},{5,6},{7,8},{9,10},{11,12},{13,14},{2,1},{4,3},{6,5},{... | collective-permute-start | bytes 663560 | tf_op jit(solution)/shard_map/ppermute | solution.py:322
  65.5 0.0 collective-permute-done.1.inner_ref
  65.6 15.5 %collective-permute-done.outer_ref = f32[3,24,768]{2,1,0:T(8,128)S(1)} collective-permute-done((f32[3,24,768]{2,1,0:T(8,128)S(1)}, f32[3,24,768]{2,1,0:T(8,128)S(1)}, u32[]{:S(2)}, u32[]{:S(2)}) %collective-permute-start) | collective-permute-done | bytes 221216 | tf_op jit(solution)/shard_map/ppermute | solution.py:322
  81.0 0.8 shard_map.32
Async XLA Ops:
  0.0 1.0 %copy-start = (f32[4,24,768]{2,1,0:T(8,128)S(1)}, f32[4,24,768]{2,1,0:T(8,128)}, u32[]{:S(2)}) copy-start(f32[4,24,768]{2,1,0:T(8,128)} %s_ref.1) | copy-start | bytes 884740
  1.0 0.9 %copy-start.1 = (f32[3,64,8,16]{1,3,2,0:T(8,128)S(1)}, f32[3,64,8,16]{1,3,2,0:T(8,128)}, u32[]{:S(2)}) copy-start(f32[3,64,8,16]{1,3,2,0:T(8,128)} %param.3) | copy-start | bytes 294916
  59.0 6.5 %collective-permute-start.1 = (f32[3,24,768]{2,1,0:T(8,128)S(1)}, f32[3,24,768]{2,1,0:T(8,128)S(1)}, u32[]{:S(2)}, u32[]{:S(2)}) collective-permute-start(f32[3,24,768]{2,1,0:T(8,128)S(1)} %get-tuple-element.28), channel_id=1, source_target_pairs={{0,1},{2,3},{4,5},{6,7},{8,9},{10,11},{12,13},{14,15},{1,0},{3,2},... | collective-permute-start | bytes 663560 | tf_op jit(solution)/shard_map/ppermute | solution.py:325
  62.9 18.1 %collective-permute-start = (f32[3,24,768]{2,1,0:T(8,128)S(1)}, f32[3,24,768]{2,1,0:T(8,128)S(1)}, u32[]{:S(2)}, u32[]{:S(2)}) collective-permute-start(f32[3,24,768]{2,1,0:T(8,128)S(1)} %get-tuple-element.27), channel_id=1, source_target_pairs={{1,2},{3,4},{5,6},{7,8},{9,10},{11,12},{13,14},{2,1},{4,3},{6,5},{... | collective-permute-start | bytes 663560 | tf_op jit(solution)/shard_map/ppermute | solution.py:322

commit v5 on v3

--- a/solution.py
+++ b/solution.py
@@ -68,7 +68,7 @@
     return x
 
 
-def pack_velocity(v_ref, out_ref):
+def pack_velocity(v_ref, after_ref, out_ref):
     lane = iota((8, 128), 1)
     tiles = []
     for c in range(3):
@@ -93,51 +93,47 @@
     return lax.axis_index("gz") & 1
 
 
-def pack_scalar(s_ref, out_ref, t_ref):
+def pack_chunks(s_ref, r_ref, out_ref, t_ref):
     flip = odd_device() * 3
     for v in range(6):
         part = slice(128 * v, 128 * v + 128)
         block = jnp.concatenate([s_ref[p ^ flip, :, part] for p in range(4)] + [jnp.zeros((32, 128), F32)], axis=0)
         t_ref[part, :] = block.T
+    shape = (16, 8, 128)
+    lane = iota(shape, 2)
+    col = lane & 15
+    slot = lane >> 4
+
+    def block(x, step):
+        return jnp.concatenate([x[step:], x[:step]], axis=0)
+
+    here, depth = r_ref[:, 0:8, :], r_ref[:, 8:16, :]
+    wide = jnp.where(col == 0, block(roll(here, -15, 2), -1), roll(here, 1, 2))
+    even = (wide, here, depth)
+    wide = jnp.where(col < 9, roll(here, -7, 2), block(roll(here, 9, 2), 1))
+    near = jnp.where(col < 8, roll(here, -8, 2), block(roll(here, 8, 2), 1))
+    depth = jnp.where(col < 8, roll(depth, -8, 2), block(roll(depth, 8, 2), 1))
+    stash = []
+    for parity, (wide, near, depth) in enumerate((even, (wide, near, depth))):
+        tile = jnp.where(slot < 4, wide, near)
+        tile = jnp.where((slot >= 4) & (col >= 9), roll(depth, 73, 2), tile)
+        tile = jnp.where((slot < 2) & (col >= 11), roll(depth, -53, 2), tile)
+        tile = jnp.where(((slot >> 1) == 1) & (col >= 11), roll(depth, -26, 2), tile)
+        rest = jnp.where((slot < 4) & ((col == 7) | (col == 8)), depth, 0.0)
+        for bit in (4, 2, 1):
+            rest = rest + roll(roll(rest, -bit, 1), 2 * bit, 2)
+        stash.append(roll(rest, 3, 1))
+        for n in range(16):
+            out_ref[2 * n + parity, 24:32, :] = tile[n]
     lane = iota((8, 128), 1)
     row = iota((8, 128), 0)
     for i in range(32):
         left = t_ref[(24 * i - 8) % 768 : (24 * i - 8) % 768 + 8, :]
         right = t_ref[(24 * i + 24) % 768 : (24 * i + 24) % 768 + 8, :]
-        halo = jnp.where(row < 4, right, left)
+        halo = jnp.where(row < 3, right, jnp.where(row == 3, stash[i % 2][i // 2], left))
         for t in range(3):
             tile = t_ref[24 * i + 8 * t : 24 * i + 8 * t + 8, :]
             out_ref[i, 8 * t : 8 * t + 8, :] = jnp.where(lane < 96, tile, roll(halo, 96 - 32 * t, 1))
-
-
-def add_velocity(old_ref, r_ref, out_ref):
-    lane = iota((8, 128), 1)
-    row = iota((8, 128), 0)
-    col = lane & 15
-    slot = lane >> 4
-    for i in range(32):
-        k = i // 2
-        here, depth = r_ref[k, 0:8, :], r_ref[k, 8:16, :]
-        if i % 2 == 0:
-            other = r_ref[(k - 1) % 16, 0:8, :]
-            wide = jnp.where(col == 0, roll(other, -15, 1), roll(here, 1, 1))
-            near = here
-        else:
-            other = r_ref[(k + 1) % 16, 0:8, :]
-            wide = jnp.where(col < 9, roll(here, -7, 1), roll(other, 9, 1))
-            near = jnp.where(col < 8, roll(here, -8, 1), roll(other, 8, 1))
-            depth = jnp.where(col < 8, roll(depth, -8, 1), roll(r_ref[(k + 1) % 16, 8:16, :], 8, 1))
-        tile = jnp.where(slot < 4, wide, near)
-        tile = jnp.where((slot >= 4) & (col >= 9), roll(depth, 73, 1), tile)
-        tile = jnp.where((slot < 2) & (col >= 11), roll(depth, -53, 1), tile)
-        tile = jnp.where(((slot >> 1) == 1) & (col >= 11), roll(depth, -26, 1), tile)
-        out_ref[i, 24:32, :] = tile
-        rest = jnp.where((slot < 4) & ((col == 7) | (col == 8)), depth, 0.0)
-        rest = pltpu.roll(rest, 0, 1, stride=2, stride_axis=0)
-        stash = jnp.broadcast_to(jnp.sum(rest, axis=0, keepdims=True), (8, 128))
-        for t in range(3):
-            rows = slice(8 * t, 8 * t + 8)
-            out_ref[i, rows, :] = jnp.where((row == 3) & (lane >= 96), roll(stash, 96 - 32 * t, 1), old_ref[i, rows, :])
 
 
 def hat_rows(rows, slot, ring):
@@ -176,30 +172,31 @@
     return jnp.concatenate([hi, (x - hi.astype(F32)).astype(BF16)], axis=0)
 
 
-def unpack(s_ref, f_ref, c_ref, planes):
-    lane = iota((8, 128), 1)
-    row = iota((8, 128), 0)
+def unpack(s_ref, f_ref, c_ref, h_ref, planes):
+    shape = (32, 8, 128)
+    lane = iota(shape, 2)
+    row = iota(shape, 1)
     col = lane & 15
     slot = lane >> 4
+    parts = [roll(s_ref[:, 8 * t : 8 * t + 8, :], 32 * t - 96, 2) for t in range(3)]
+    halo = jnp.where(lane < 32, parts[0], jnp.where(lane < 64, parts[1], parts[2]))
+    h_ref[...] = halo
+    packed = s_ref[:, 24:32, :]
+    c_ref[0] = packed.reshape(256, 128) * (1.0 / 9.0)
+    rest = jnp.broadcast_to(halo[:, 3:4, :], shape)
+    for bit in (1, 2, 4):
+        rest = jnp.where((row & bit) == 0, rest, roll(rest, -2 * bit, 2))
+    depth = jnp.where(slot >= 4, jnp.where(col < 5, roll(packed, 53, 2), roll(packed, 26, 2)), jnp.where(col < 7, roll(packed, -73, 2), rest))
+    c_ref[1] = depth.reshape(256, 128) * (1.0 / 9.0)
     for i in range(32):
-        tiles = [s_ref[i, 8 * t : 8 * t + 8, :] for t in range(3)]
-        halo = jnp.where(lane < 32, roll(tiles[0], -96, 1), jnp.where(lane < 64, roll(tiles[1], -64, 1), roll(tiles[2], -32, 1)))
+        whole = jnp.concatenate([s_ref[i, 0:24, :], h_ref[i]], axis=0)
         v, at = divmod(24 * i, 128)
         here = min(24, 128 - at)
-        for t, tile in enumerate(tiles + [halo]):
-            rows = slice(8 * t, 8 * t + 8)
-            for n, p in enumerate(planes):
-                moved = roll(tile, at - 24 * p, 1)
-                f_ref[n, rows, 128 * v + at : 128 * v + at + here] = moved[:, at : at + here]
-                if here < 24:
-                    f_ref[n, rows, 128 * v + 128 : 128 * v + 128 + 24 - here] = moved[:, : 24 - here]
-        packed = s_ref[i, 24:32, :]
-        rest = jnp.broadcast_to(halo[3:4, :], (8, 128))
-        for bit in (1, 2, 4):
-            rest = jnp.where((row & bit) == 0, rest, roll(rest, -2 * bit, 1))
-        depth = jnp.where(slot >= 4, jnp.where(col < 5, roll(packed, 53, 1), roll(packed, 26, 1)), jnp.where(col < 7, roll(packed, -73, 1), rest))
-        c_ref[0, 8 * i : 8 * i + 8, :] = packed * (1.0 / 9.0)
-        c_ref[1, 8 * i : 8 * i + 8, :] = depth * (1.0 / 9.0)
+        for n, p in enumerate(planes):
+            moved = roll(whole, at - 24 * p, 1)
+            f_ref[n, :, 128 * v + at : 128 * v + at + here] = moved[:, at : at + here]
+            if here < 24:
+                f_ref[n, :, 128 * v + 128 : 128 * v + 128 + 24 - here] = moved[:, : 24 - here]
 
 
 def refine(coarse, y_ref, hats_ref):
@@ -226,8 +223,8 @@
     lax.fori_loop(0, 3, along_y, 0)
 
 
-def near_planes(s_ref, y_ref, hats_ref, hats_z_ref, outer_ref, own_ref, inner_ref, f_ref, c_ref, u_ref, w_ref, x_ref, q_ref):
-    unpack(s_ref, f_ref, c_ref, (0, 1, 2))
+def near_planes(s_ref, y_ref, hats_ref, hats_z_ref, outer_ref, own_ref, inner_ref, f_ref, c_ref, h_ref, u_ref, w_ref, x_ref, q_ref):
+    unpack(s_ref, f_ref, c_ref, h_ref, (0, 1, 2))
     u_ref[...] = refine(c_ref[0], y_ref, hats_ref)
     w_ref[...] = refine(c_ref[1], y_ref, hats_z_ref)
     plane_sweeps(f_ref, u_ref, x_ref, q_ref, 3)
@@ -253,8 +250,8 @@
     lax.fori_loop(0, 6, along_z, 0)
 
 
-def far_plane(s_ref, y_ref, hats_ref, hats_z_ref, some_ref, rest_ref, own_ref, inner_ref, f_ref, c_ref, u_ref, w_ref, x_ref, q_ref):
-    unpack(s_ref, f_ref, c_ref, (3,))
+def far_plane(s_ref, y_ref, hats_ref, hats_z_ref, some_ref, rest_ref, own_ref, inner_ref, f_ref, c_ref, h_ref, u_ref, w_ref, x_ref, q_ref):
+    unpack(s_ref, f_ref, c_ref, h_ref, (3,))
     u_ref[...] = refine(c_ref[0], y_ref, hats_ref)
     w_ref[...] = refine(c_ref[1], y_ref, hats_z_ref)
     plane_sweeps(f_ref, u_ref, x_ref, q_ref, 1)
@@ -283,15 +280,16 @@
     out_ref[3 ^ flip] = own_ref[3] + inner_ref[0]
 
 
-def kernel(body, *shapes, scratch=(), alias=None, flops=1e7):
+def kernel(body, *shapes, scratch=(), flops=1e7, specs=None):
     outs = tuple(jax.ShapeDtypeStruct(*(s if isinstance(s[0], tuple) else (s, F32))) for s in shapes)
+    extra = {"in_specs": [pl.BlockSpec(memory_space=m) for m in specs]} if specs else {}
     return pl.pallas_call(
         body,
         out_shape=outs if len(outs) > 1 else outs[0],
         scratch_shapes=[pltpu.VMEM(s, F32) for s in scratch],
-        input_output_aliases=alias or {},
         cost_estimate=pl.CostEstimate(flops=int(flops), transcendentals=0, bytes_accessed=1 << 20),
         compiler_params=pltpu.CompilerParams(vmem_limit_bytes=16 * 1024 * 1024),
+        **extra,
     )
 
 
@@ -300,15 +298,15 @@
 
 
 def sweep_scratch(count, speeds):
-    return [(count, 32, 768), (2, 256, 128), (56 * count, 768), (24 * speeds, 768), (count, 24, 768), (count, 24, 768)]
+    return [(count, 32, 768), (2, 256, 128), (32, 8, 128), (56 * count, 768), (24 * speeds, 768), (count, 24, 768), (count, 24, 768)]
 
 
 def steps(scalar, velocity):
-    planes = exchange(kernel(pack_velocity, (16, 16, 128))(jnp.transpose(velocity, (0, 2, 3, 1))), "gz")
-    chunks = kernel(pack_scalar, (32, 32, 128), scratch=[(768, 128)])(scalar)
-    tables = ((256, 768), (168, 256), (120, 256), (56, 256), (72, 256))
-    y_weights, near, near_z, far, far_z = kernel(weights, *((s, BF16) for s in tables))()
-    chunks = exchange(kernel(add_velocity, (32, 32, 128), alias={0: 0})(chunks, planes), "gy")
+    tables = [(t, BF16) for t in ((256, 768), (168, 256), (120, 256), (56, 256), (72, 256))]
+    y_weights, near, near_z, far, far_z = kernel(weights, *tables)()
+    coarse = jnp.transpose(velocity, (0, 2, 3, 1))
+    planes = exchange(kernel(pack_velocity, (16, 16, 128), specs=(pltpu.VMEM, pl.ANY))(coarse, near), "gz")
+    chunks = exchange(kernel(pack_chunks, (32, 32, 128), scratch=[(768, 128)])(scalar, planes), "gy")
     outer, own, inner = kernel(near_planes, (3, 24, 768), (4, 24, 768), (2, 24, 768), scratch=sweep_scratch(3, 5))(chunks, y_weights, near, near_z)
     count = lax.axis_size("gz")
     pairs = [(k, k + 1) for k in range(1, count - 1, 2)]

time: 82.3 us -> 78 us (0.948)
  blocking collectives: 0 us -> 47.1 us
  waiting for transfers between devices: 39.4 us -> 15.5 us
  starting transfers between devices: 28.5 us -> 6.49 us
  Pallas kernels: 13 us -> 7.74 us
    all_to_all x0 -> x2, blocking collectives: none -> 47.1 us  [exchange(): return lax.all_to_all(x, axis, split_axis=0, concat_axis=0, tiled=False)]
    all_to_all x2 -> x0, waiting for transfers between devices: 24 us -> none  [exchange(): return lax.all_to_all(x, axis, split_axis=0, concat_axis=0, tiled=False)]
    all_to_all x2 -> x0, starting transfers between devices: 22 us -> none  [exchange(): return lax.all_to_all(x, axis, split_axis=0, concat_axis=0, tiled=False)]
    pallas_call x4 -> x3, Pallas kernels: 6.52 us -> 1.67 us  [the longest x1 0.88 us: steps(): kernel(pack_chunks, (32, 32, 128), scratch=[(768, 128)])(scalar, planes)]
  transfers between devices with their start and end apart: 4 -> 2, of which waited for: 3 -> 1; matrix products, arithmetic and copies ran while one was open for 0% -> 0% of each run, Pallas kernels for 2% -> 0%
where the time goes in v5:
time: 78 us; the launch traced here: 77.8 us
  blocking collectives  47.1 us (60%)
  waiting for transfers between devices  15.5 us (20%)
  Pallas kernels  7.74 us (10%)
  starting transfers between devices  6.49 us (8%)
  local copies, waits for them, and re-layouts  0.93 us (1%)
    all_to_all x2, blocking collectives, exchange(): return lax.all_to_all(x, axis, split_axis=0, concat_axis=0, tiled=False)  47.1 us
    ppermute x1, waiting for transfers between devices, steps(): outer = lax.ppermute(outer, 'gz', pairs + [(b, a) for a, b in pairs])  15.5 us
    ppermute x1, starting transfers between devices, steps(): inner = lax.ppermute(inner, 'gz', pairs + [(b, a) for a, b in pairs])  3.83 us
    pallas_call x1, Pallas kernels, steps(): kernel(near_planes, (3, 24, 768), (4, 24, 768), (2, 24, 768), scratch=swe...  3.18 us
    ppermute x1, starting transfers between devices, steps(): outer = lax.ppermute(outer, 'gz', pairs + [(b, a) for a, b in pairs])  2.66 us
    pallas_call x1, Pallas kernels, steps(): kernel(far_plane, (4, 24, 768), (3, 24, 768), scratch=sweep_scratch(1, 3)...  2.12 us
  transfers between devices with their start and end apart: 2, of which 1 were waited for; matrix products, arithmetic and copies ran while one was open for 0% of the time, Pallas kernels for 0%

profile of v5, /device:TPU:17, one launch (start us, length us, event | category | flops | bytes accessed | tf_op | source)
XLA Modules:
  0.0 77.8 jit_solution(6586235064898425286)
XLA Ops:
  0.0 0.3 shard_map.28
  0.3 0.0 copy-start.1
  0.3 0.9 %copy-done.1 = f32[3,64,8,16]{1,3,2,0:T(8,128)S(1)} copy-done((f32[3,64,8,16]{1,3,2,0:T(8,128)S(1)}, f32[3,64,8,16]{1,3,2,0:T(8,128)}, u32[]{:S(2)}) %copy-start.1) | copy-done | bytes 98328
  1.3 0.0 copy-start
  1.3 0.5 shard_map.29
  1.7 18.3 %all_to_all.10.r_ref = f32[16,16,128]{2,1,0:T(8,128)S(1)} all-to-all(f32[16,16,128]{2,1,0:T(8,128)S(1)} %shard_map.29), channel_id=1, replica_groups=mesh['gy'=32,'gz'=16] {'gz'}, dimensions={0} | all-to-all | bytes 262144 | tf_op jit(solution)/shard_map/all_to_all | solution.py:297
  20.0 0.0 copy-done
  20.0 0.9 %shard_map.30 = f32[32,32,128]{2,1,0:T(8,128)S(1)} custom-call(f32[4,24,768]{2,1,0:T(8,128)S(1)} %copy-done, f32[16,16,128]{2,1,0:T(8,128)S(1)} %all_to_all.10.r_ref), custom_call_target="tpu_custom_call" | custom-call | flops 10000000 | bytes 1048576 | tf_op jit(solution)/shard_map/pallas_call | solution.py:309
  20.9 28.8 %all_to_all.11.s_ref = f32[32,32,128]{2,1,0:T(8,128)S(1)} all-to-all(f32[32,32,128]{2,1,0:T(8,128)S(1)} %shard_map.30), channel_id=1, replica_groups=mesh['gy'=32,'gz'=16] {'gy'}, dimensions={0} | all-to-all | bytes 1048576 | tf_op jit(solution)/shard_map/all_to_all | solution.py:297
  49.7 3.2 %shard_map.31 = (f32[3,24,768]{2,1,0:T(8,128)S(1)}, f32[4,24,768]{2,1,0:T(8,128)S(1)}, f32[2,24,768]{2,1,0:T(8,128)S(1)}) custom-call(f32[32,32,128]{2,1,0:T(8,128)S(1)} %all_to_all.11.s_ref, bf16[256,768]{1,0:T(8,128)(2,1)S(1)} %get-tuple-element.16.y_ref, bf16[168,256]{1,0:T(8,128)(2,1)S(1)} %get-tuple-element.15.after_ref.hats_ref, ...), custom_call_target="tpu_custom_call" | custom-call | flops 10000000 | bytes 1048576 | tf_op jit(solution)/shard_map/pallas_call | solution.py:310
  52.9 2.1 %shard_map.32 = (f32[4,24,768]{2,1,0:T(8,128)S(1)}, f32[3,24,768]{2,1,0:T(8,128)S(1)}) custom-call(f32[32,32,128]{2,1,0:T(8,128)S(1)} %all_to_all.11.s_ref, bf16[256,768]{1,0:T(8,128)(2,1)S(1)} %get-tuple-element.16.y_ref, bf16[56,256]{1,0:T(8,128)(2,1)S(1)} %get-tuple-element.17.hats_ref, bf16[72,256]{1,0:T(8,128)(2,1)S(1)} %get-tuple-element.18.hats_z_ref, ...), custom_call_target="tpu_custom_call" | custom-call | flops 1000000000 | bytes 1048576 | tf_op jit(solution)/shard_map/pallas_call | solution.py:314
  55.0 3.8 %collective-permute-start.1 = (f32[3,24,768]{2,1,0:T(8,128)S(1)}, f32[3,24,768]{2,1,0:T(8,128)S(1)}, u32[]{:S(2)}, u32[]{:S(2)}) collective-permute-start(f32[3,24,768]{2,1,0:T(8,128)S(1)} %get-tuple-element.24), channel_id=1, source_target_pairs={{0,1},{2,3},{4,5},{6,7},{8,9},{10,11},{12,13},{14,15},{1,0},{3,2},... | collective-permute-start | bytes 663560 | tf_op jit(solution)/shard_map/ppermute | solution.py:316
  58.9 2.7 %collective-permute-start = (f32[3,24,768]{2,1,0:T(8,128)S(1)}, f32[3,24,768]{2,1,0:T(8,128)S(1)}, u32[]{:S(2)}, u32[]{:S(2)}) collective-permute-start(f32[3,24,768]{2,1,0:T(8,128)S(1)} %get-tuple-element.23), channel_id=1, source_target_pairs={{1,2},{3,4},{5,6},{7,8},{9,10},{11,12},{13,14},{2,1},{4,3},{6,5},{... | collective-permute-start | bytes 663560 | tf_op jit(solution)/shard_map/ppermute | solution.py:313
  61.5 0.0 collective-permute-done.1.inner_ref
  61.5 15.5 %collective-permute-done.outer_ref = f32[3,24,768]{2,1,0:T(8,128)S(1)} collective-permute-done((f32[3,24,768]{2,1,0:T(8,128)S(1)}, f32[3,24,768]{2,1,0:T(8,128)S(1)}, u32[]{:S(2)}, u32[]{:S(2)}) %collective-permute-start) | collective-permute-done | bytes 221216 | tf_op jit(solution)/shard_map/ppermute | solution.py:313
  77.0 0.8 shard_map.33
Async XLA Ops:
  0.3 0.9 %copy-start.1 = (f32[3,64,8,16]{1,3,2,0:T(8,128)S(1)}, f32[3,64,8,16]{1,3,2,0:T(8,128)}, u32[]{:S(2)}) copy-start(f32[3,64,8,16]{1,3,2,0:T(8,128)} %param.3) | copy-start | bytes 294916
  1.3 18.7 %copy-start = (f32[4,24,768]{2,1,0:T(8,128)S(1)}, f32[4,24,768]{2,1,0:T(8,128)}, u32[]{:S(2)}) copy-start(f32[4,24,768]{2,1,0:T(8,128)} %s_ref.1) | copy-start | bytes 884740
  55.0 6.5 %collective-permute-start.1 = (f32[3,24,768]{2,1,0:T(8,128)S(1)}, f32[3,24,768]{2,1,0:T(8,128)S(1)}, u32[]{:S(2)}, u32[]{:S(2)}) collective-permute-start(f32[3,24,768]{2,1,0:T(8,128)S(1)} %get-tuple-element.24), channel_id=1, source_target_pairs={{0,1},{2,3},{4,5},{6,7},{8,9},{10,11},{12,13},{14,15},{1,0},{3,2},... | collective-permute-start | bytes 663560 | tf_op jit(solution)/shard_map/ppermute | solution.py:316
  58.9 18.1 %collective-permute-start = (f32[3,24,768]{2,1,0:T(8,128)S(1)}, f32[3,24,768]{2,1,0:T(8,128)S(1)}, u32[]{:S(2)}, u32[]{:S(2)}) collective-permute-start(f32[3,24,768]{2,1,0:T(8,128)S(1)} %get-tuple-element.23), channel_id=1, source_target_pairs={{1,2},{3,4},{5,6},{7,8},{9,10},{11,12},{13,14},{2,1},{4,3},{6,5},{... | collective-permute-start | bytes 663560 | tf_op jit(solution)/shard_map/ppermute | solution.py:313

commit v6 on v5

--- a/solution.py
+++ b/solution.py
@@ -20,12 +20,15 @@
     a = size - (0.5 * size) * (size - jnp.where(up, after, -before))
     b = a - 0.5
     s = b * b
-    e1 = (-1.0 / 16.0 * s + 13.0 / 32.0) * s - 25.0 / 256.0
-    e2 = (1.0 / 48.0 * s - 5.0 / 96.0) * s + 3.0 / 256.0
-    e0 = 0.5 - e1 - e2
-    o0 = ((-25.0 / 12.0 * s + 19.0 / 8.0) * s - 281.0 / 192.0) * b
-    o1 = ((25.0 / 24.0 * s - 53.0 / 48.0) * s + 27.0 / 128.0) * b
-    o2 = ((-5.0 / 24.0 * s + 3.0 / 16.0) * s - 13.0 / 384.0) * b
+    g1, g3, g5 = s - 0.25, s - 2.25, s - 6.25
+    e2 = g1 * g3
+    e1 = (g1 * g5) * -3.0
+    e0 = (g3 * g5) * 2.0
+    g = g1 * b
+    o2 = g * (6.5 - 10.0 * s)
+    o1 = g * (50.0 * s - 40.5)
+    o0 = g * (89.0 - 100.0 * s) - 48.0 * b
+    q = q * (1.0 / 48.0)
     at0 = q * (e0 + o0)
     near1, far1 = q * (e0 - o0), q * (e1 + o1)
     near2, far2 = q * (e1 - o1), q * (e2 + o2)
@@ -158,7 +161,7 @@
         return jnp.concatenate(rows, axis=0).astype(F32).astype(BF16)
 
     sign = 1 - 2 * odd
-    for planes, speeds, xy_ref, z_ref in (((0, 1, 2), range(5), near_ref, near_z_ref), ((3,), (3, 4, 5), far_ref, far_z_ref)):
+    for planes, speeds, xy_ref, z_ref in (((0, 1, 2), range(5), near_ref, near_z_ref), ((3,), range(6), far_ref, far_z_ref)):
         xy = both([hat_rows(32, p ^ (3 * odd), True) for p in planes] + [hat_rows(24, 4 + (p ^ (3 * odd)), False) for p in planes])
         z = both([hat_rows(24, jnp.where(odd == 1, 5 - p, p), False) * sign for p in speeds])
         xy_ref[:, 0:128] = xy
@@ -223,7 +226,7 @@
     lax.fori_loop(0, 3, along_y, 0)
 
 
-def near_planes(s_ref, y_ref, hats_ref, hats_z_ref, outer_ref, own_ref, inner_ref, f_ref, c_ref, h_ref, u_ref, w_ref, x_ref, q_ref):
+def near_planes(s_ref, y_ref, hats_ref, hats_z_ref, outer_ref, q_ref, f_ref, c_ref, h_ref, u_ref, w_ref, x_ref):
     unpack(s_ref, f_ref, c_ref, h_ref, (0, 1, 2))
     u_ref[...] = refine(c_ref[0], y_ref, hats_ref)
     w_ref[...] = refine(c_ref[1], y_ref, hats_z_ref)
@@ -234,23 +237,16 @@
         for t in range(3):
             rows = slice(8 * t, 8 * t + 8)
             speeds = [w_ref[24 * p + 8 * t : 24 * p + 8 * t + 8, part] for p in range(5)]
-            total = {}
-            for p in range(3):
-                terms = remesh_terms(speeds[p + 1], speeds[p], speeds[p + 2], q_ref[p, rows, part])
-                for m, term in terms.items():
-                    total[p + m] = total[p + m] + term if p + m in total else term
-            for n in range(3):
-                outer_ref[n, rows, part] = total[-1 - n]
-            for n in range(4):
-                own_ref[n, rows, part] = total[n]
-            for n in range(2):
-                inner_ref[n, rows, part] = total[4 + n]
+            first, second, third = [remesh_terms(speeds[p + 1], speeds[p], speeds[p + 2], q_ref[p, rows, part]) for p in range(3)]
+            outer_ref[0, rows, part] = first[-1] + second[-2] + third[-3]
+            outer_ref[1, rows, part] = first[-2] + second[-3]
+            outer_ref[2, rows, part] = first[-3]
         return carry
 
     lax.fori_loop(0, 6, along_z, 0)
 
 
-def far_plane(s_ref, y_ref, hats_ref, hats_z_ref, some_ref, rest_ref, own_ref, inner_ref, f_ref, c_ref, h_ref, u_ref, w_ref, x_ref, q_ref):
+def far_plane(s_ref, y_ref, hats_ref, hats_z_ref, near_ref, own_ref, inner_ref, f_ref, c_ref, h_ref, u_ref, w_ref, x_ref, q_ref):
     unpack(s_ref, f_ref, c_ref, h_ref, (3,))
     u_ref[...] = refine(c_ref[0], y_ref, hats_ref)
     w_ref[...] = refine(c_ref[1], y_ref, hats_z_ref)
@@ -260,13 +256,17 @@
         part = pl.ds(pl.multiple_of(128 * v, 128), 128)
         for t in range(3):
             rows = slice(8 * t, 8 * t + 8)
-            before, speed, after = [w_ref[24 * p + 8 * t : 24 * p + 8 * t + 8, part] for p in range(3)]
-            terms = remesh_terms(speed, before, after, q_ref[0, rows, part])
+            speeds = [w_ref[24 * p + 8 * t : 24 * p + 8 * t + 8, part] for p in range(6)]
+            total = {}
+            for p in range(4):
+                q = q_ref[0, rows, part] if p == 3 else near_ref[p, rows, part]
+                terms = remesh_terms(speeds[p + 1], speeds[p], speeds[p + 2], q)
+                for m, term in terms.items():
+                    total[p + m] = total[p + m] + term if p + m in total else term
             for n in range(4):
-                own_ref[n, rows, part] = some_ref[n, rows, part] + terms[n - 3]
-            for n in range(2):
-                inner_ref[n, rows, part] = rest_ref[n, rows, part] + terms[1 + n]
-            inner_ref[2, rows, part] = terms[3]
+                own_ref[n, rows, part] = total[n]
+            for n in range(3):
+                inner_ref[n, rows, part] = total[4 + n]
         return carry
 
     lax.fori_loop(0, 6, along_z, 0)
@@ -298,20 +298,20 @@
 
 
 def sweep_scratch(count, speeds):
-    return [(count, 32, 768), (2, 256, 128), (32, 8, 128), (56 * count, 768), (24 * speeds, 768), (count, 24, 768), (count, 24, 768)]
+    return [(count, 32, 768), (2, 256, 128), (32, 8, 128), (56 * count, 768), (24 * speeds, 768), (count, 24, 768)]
 
 
 def steps(scalar, velocity):
-    tables = [(t, BF16) for t in ((256, 768), (168, 256), (120, 256), (56, 256), (72, 256))]
-    y_weights, near, near_z, far, far_z = kernel(weights, *tables)()
+    tables = [(t, BF16) for t in ((256, 768), (168, 256), (120, 256), (56, 256), (144, 256))]
+    y_weights, near, near_z, far, far_z = kernel(weights, *tables, flops=1e9)()
     coarse = jnp.transpose(velocity, (0, 2, 3, 1))
     planes = exchange(kernel(pack_velocity, (16, 16, 128), specs=(pltpu.VMEM, pl.ANY))(coarse, near), "gz")
     chunks = exchange(kernel(pack_chunks, (32, 32, 128), scratch=[(768, 128)])(scalar, planes), "gy")
-    outer, own, inner = kernel(near_planes, (3, 24, 768), (4, 24, 768), (2, 24, 768), scratch=sweep_scratch(3, 5))(chunks, y_weights, near, near_z)
+    outer, swept = kernel(near_planes, (3, 24, 768), (3, 24, 768), scratch=sweep_scratch(3, 5))(chunks, y_weights, near, near_z)
     count = lax.axis_size("gz")
     pairs = [(k, k + 1) for k in range(1, count - 1, 2)]
     outer = lax.ppermute(outer, "gz", pairs + [(b, a) for a, b in pairs])
-    own, inner = kernel(far_plane, (4, 24, 768), (3, 24, 768), scratch=sweep_scratch(1, 3), flops=1e9)(chunks, y_weights, far, far_z, own, inner)
+    own, inner = kernel(far_plane, (4, 24, 768), (3, 24, 768), scratch=sweep_scratch(1, 6) + [(1, 24, 768)], flops=1e9)(chunks, y_weights, far, far_z, swept)
     pairs = [(k, k + 1) for k in range(0, count, 2)]
     inner = lax.ppermute(inner, "gz", pairs + [(b, a) for a, b in pairs])
     return kernel(join, (4, 24, 768))(own, outer, inner)

time: 78 us -> 77.7 us (level)
  no operation moved by 1% of the time
where the time goes in v6:
time: 77.7 us; the launch traced here: 77.5 us
  blocking collectives  47.1 us (61%)
  waiting for transfers between devices  15.5 us (20%)
  Pallas kernels  7.84 us (10%)
  starting transfers between devices  6.5 us (8%)
    all_to_all x2, blocking collectives, exchange(): return lax.all_to_all(x, axis, split_axis=0, concat_axis=0, tiled=False)  47.1 us
    ppermute x1, waiting for transfers between devices, steps(): outer = lax.ppermute(outer, 'gz', pairs + [(b, a) for a, b in pairs])  15.5 us
    ppermute x1, starting transfers between devices, steps(): inner = lax.ppermute(inner, 'gz', pairs + [(b, a) for a, b in pairs])  3.83 us
    pallas_call x1, Pallas kernels, steps(): kernel(near_planes, (3, 24, 768), (3, 24, 768), scratch=sweep_scratch(3, 5))  2.93 us
    ppermute x1, starting transfers between devices, steps(): outer = lax.ppermute(outer, 'gz', pairs + [(b, a) for a, b in pairs])  2.67 us
    pallas_call x1, Pallas kernels, steps(): kernel(far_plane, (4, 24, 768), (3, 24, 768), scratch=sweep_scratch(1, 6)...  2.46 us
  transfers between devices with their start and end apart: 2, of which 1 were waited for; matrix products, arithmetic and copies ran while one was open for 0% of the time, Pallas kernels for 0%

profile of v6, /device:TPU:17, one launch (start us, length us, event | category | flops | bytes accessed | tf_op | source)
XLA Modules:
  0.0 77.5 jit_solution(12324854318727110869)
XLA Ops:
  0.0 0.0 copy-start.1
  0.0 0.3 shard_map.28
  0.3 0.6 copy-done.1
  0.9 0.0 copy-start
  0.9 0.5 shard_map.29
  1.4 18.3 %all_to_all.10.r_ref = f32[16,16,128]{2,1,0:T(8,128)S(1)} all-to-all(f32[16,16,128]{2,1,0:T(8,128)S(1)} %shard_map.29), channel_id=1, replica_groups=mesh['gy'=32,'gz'=16] {'gz'}, dimensions={0} | all-to-all | bytes 262144 | tf_op jit(solution)/shard_map/all_to_all | solution.py:297
  19.7 0.0 copy-done
  19.7 0.9 %shard_map.30 = f32[32,32,128]{2,1,0:T(8,128)S(1)} custom-call(f32[4,24,768]{2,1,0:T(8,128)S(1)} %copy-done, f32[16,16,128]{2,1,0:T(8,128)S(1)} %all_to_all.10.r_ref), custom_call_target="tpu_custom_call" | custom-call | flops 10000000 | bytes 1048576 | tf_op jit(solution)/shard_map/pallas_call | solution.py:309
  20.6 28.8 %all_to_all.11.s_ref = f32[32,32,128]{2,1,0:T(8,128)S(1)} all-to-all(f32[32,32,128]{2,1,0:T(8,128)S(1)} %shard_map.30), channel_id=1, replica_groups=mesh['gy'=32,'gz'=16] {'gy'}, dimensions={0} | all-to-all | bytes 1048576 | tf_op jit(solution)/shard_map/all_to_all | solution.py:297
  49.4 2.9 %shard_map.31 = (f32[3,24,768]{2,1,0:T(8,128)S(1)}, f32[3,24,768]{2,1,0:T(8,128)S(1)}) custom-call(f32[32,32,128]{2,1,0:T(8,128)S(1)} %all_to_all.11.s_ref, bf16[256,768]{1,0:T(8,128)(2,1)S(1)} %get-tuple-element.15.y_ref, bf16[168,256]{1,0:T(8,128)(2,1)S(1)} %get-tuple-element.14.after_ref.hats_ref, bf16[120,256]{1,0:T(8,128)(2,1)S(1)} %get-tuple-element.18.hats_z_ref), custom_call_target="tpu_custom_call" | custom-call | flops 10000000 | bytes 1048576 | tf_op jit(solution)/shard_map/pallas_call | solution.py:310
  52.3 2.5 %shard_map.32 = (f32[4,24,768]{2,1,0:T(8,128)S(1)}, f32[3,24,768]{2,1,0:T(8,128)S(1)}) custom-call(f32[32,32,128]{2,1,0:T(8,128)S(1)} %all_to_all.11.s_ref, bf16[256,768]{1,0:T(8,128)(2,1)S(1)} %get-tuple-element.15.y_ref, bf16[56,256]{1,0:T(8,128)(2,1)S(1)} %get-tuple-element.16.hats_ref, bf16[144,256]{1,0:T(8,128)(2,1)S(1)} %get-tuple-element.17.hats_z_ref, ...), custom_call_target="tpu_custom_call" | custom-call | flops 1000000000 | bytes 1048576 | tf_op jit(solution)/shard_map/pallas_call | solution.py:314
  54.8 3.8 %collective-permute-start.1 = (f32[3,24,768]{2,1,0:T(8,128)S(1)}, f32[3,24,768]{2,1,0:T(8,128)S(1)}, u32[]{:S(2)}, u32[]{:S(2)}) collective-permute-start(f32[3,24,768]{2,1,0:T(8,128)S(1)} %get-tuple-element.22), channel_id=1, source_target_pairs={{0,1},{2,3},{4,5},{6,7},{8,9},{10,11},{12,13},{14,15},{1,0},{3,2},... | collective-permute-start | bytes 663560 | tf_op jit(solution)/shard_map/ppermute | solution.py:316
  58.6 2.7 %collective-permute-start = (f32[3,24,768]{2,1,0:T(8,128)S(1)}, f32[3,24,768]{2,1,0:T(8,128)S(1)}, u32[]{:S(2)}, u32[]{:S(2)}) collective-permute-start(f32[3,24,768]{2,1,0:T(8,128)S(1)} %get-tuple-element.21), channel_id=1, source_target_pairs={{1,2},{3,4},{5,6},{7,8},{9,10},{11,12},{13,14},{2,1},{4,3},{6,5},{... | collective-permute-start | bytes 663560 | tf_op jit(solution)/shard_map/ppermute | solution.py:313
  61.3 0.0 collective-permute-done.1.inner_ref
  61.3 15.5 %collective-permute-done.outer_ref = f32[3,24,768]{2,1,0:T(8,128)S(1)} collective-permute-done((f32[3,24,768]{2,1,0:T(8,128)S(1)}, f32[3,24,768]{2,1,0:T(8,128)S(1)}, u32[]{:S(2)}, u32[]{:S(2)}) %collective-permute-start) | collective-permute-done | bytes 221216 | tf_op jit(solution)/shard_map/ppermute | solution.py:313
  76.8 0.8 shard_map.33
Async XLA Ops:
  0.0 0.9 %copy-start.1 = (f32[3,64,8,16]{1,3,2,0:T(8,128)S(1)}, f32[3,64,8,16]{1,3,2,0:T(8,128)}, u32[]{:S(2)}) copy-start(f32[3,64,8,16]{1,3,2,0:T(8,128)} %param.3) | copy-start | bytes 294916
  0.9 18.7 %copy-start = (f32[4,24,768]{2,1,0:T(8,128)S(1)}, f32[4,24,768]{2,1,0:T(8,128)}, u32[]{:S(2)}) copy-start(f32[4,24,768]{2,1,0:T(8,128)} %s_ref.1) | copy-start | bytes 884740
  54.8 6.5 %collective-permute-start.1 = (f32[3,24,768]{2,1,0:T(8,128)S(1)}, f32[3,24,768]{2,1,0:T(8,128)S(1)}, u32[]{:S(2)}, u32[]{:S(2)}) collective-permute-start(f32[3,24,768]{2,1,0:T(8,128)S(1)} %get-tuple-element.22), channel_id=1, source_target_pairs={{0,1},{2,3},{4,5},{6,7},{8,9},{10,11},{12,13},{14,15},{1,0},{3,2},... | collective-permute-start | bytes 663560 | tf_op jit(solution)/shard_map/ppermute | solution.py:316
  58.6 18.1 %collective-permute-start = (f32[3,24,768]{2,1,0:T(8,128)S(1)}, f32[3,24,768]{2,1,0:T(8,128)S(1)}, u32[]{:S(2)}, u32[]{:S(2)}) collective-permute-start(f32[3,24,768]{2,1,0:T(8,128)S(1)} %get-tuple-element.21), channel_id=1, source_target_pairs={{1,2},{3,4},{5,6},{7,8},{9,10},{11,12},{13,14},{2,1},{4,3},{6,5},{... | collective-permute-start | bytes 663560 | tf_op jit(solution)/shard_map/ppermute | solution.py:313

commit v7 on v6

--- a/solution.py
+++ b/solution.py
@@ -14,21 +14,18 @@
     return lax.broadcasted_iota(jnp.int32, shape, dim)
 
 
-def remesh_terms(u, before, after, q):
-    up = u >= 0.0
-    size = jnp.abs(u)
-    a = size - (0.5 * size) * (size - jnp.where(up, after, -before))
-    b = a - 0.5
+def remesh_terms(h, before, after, q):
+    up = h >= 0.0
+    b = jnp.abs(h - jnp.abs(h) * (h - jnp.where(up, after, before))) - 0.25
     s = b * b
-    g1, g3, g5 = s - 0.25, s - 2.25, s - 6.25
+    g1, g3, g5 = s - 1.0 / 16.0, s - 9.0 / 16.0, s - 25.0 / 16.0
     e2 = g1 * g3
     e1 = (g1 * g5) * -3.0
     e0 = (g3 * g5) * 2.0
     g = g1 * b
-    o2 = g * (6.5 - 10.0 * s)
-    o1 = g * (50.0 * s - 40.5)
-    o0 = g * (89.0 - 100.0 * s) - 48.0 * b
-    q = q * (1.0 / 48.0)
+    o2 = g * (3.25 - 20.0 * s)
+    o1 = g * (100.0 * s - 20.25)
+    o0 = g * (44.5 - 200.0 * s) - 6.0 * b
     at0 = q * (e0 + o0)
     near1, far1 = q * (e0 - o0), q * (e1 + o1)
     near2, far2 = q * (e1 - o1), q * (e2 + o2)
@@ -124,8 +121,8 @@
         tile = jnp.where(((slot >> 1) == 1) & (col >= 11), roll(depth, -26, 2), tile)
         rest = jnp.where((slot < 4) & ((col == 7) | (col == 8)), depth, 0.0)
         for bit in (4, 2, 1):
-            rest = rest + roll(roll(rest, -bit, 1), 2 * bit, 2)
-        stash.append(roll(rest, 3, 1))
+            rest = rest + roll(roll(rest, -bit, 1), -2 * bit, 2)
+        stash.append(roll(roll(rest, 3, 1), 16, 2))
         for n in range(16):
             out_ref[2 * n + parity, 24:32, :] = tile[n]
     lane = iota((8, 128), 1)
@@ -185,12 +182,11 @@
     halo = jnp.where(lane < 32, parts[0], jnp.where(lane < 64, parts[1], parts[2]))
     h_ref[...] = halo
     packed = s_ref[:, 24:32, :]
-    c_ref[0] = packed.reshape(256, 128) * (1.0 / 9.0)
-    rest = jnp.broadcast_to(halo[:, 3:4, :], shape)
-    for bit in (1, 2, 4):
-        rest = jnp.where((row & bit) == 0, rest, roll(rest, -2 * bit, 2))
+    c_ref[0] = packed.reshape(256, 128) * (1.0 / 18.0)
+    rest = jnp.broadcast_to(halo[:, 3:4, :], shape).reshape(256, 128)
+    rest = jnp.stack([pltpu.roll(rest[8 * i : 8 * i + 8], 112, 1, stride=2, stride_axis=0) for i in range(32)])
     depth = jnp.where(slot >= 4, jnp.where(col < 5, roll(packed, 53, 2), roll(packed, 26, 2)), jnp.where(col < 7, roll(packed, -73, 2), rest))
-    c_ref[1] = depth.reshape(256, 128) * (1.0 / 9.0)
+    c_ref[1] = depth.reshape(256, 128) * (1.0 / 18.0)
     for i in range(32):
         whole = jnp.concatenate([s_ref[i, 0:24, :], h_ref[i]], axis=0)
         v, at = divmod(24 * i, 128)
@@ -202,16 +198,33 @@
                 f_ref[n, :, 128 * v + 128 : 128 * v + 128 + 24 - here] = moved[:, : 24 - here]
 
 
-def refine(coarse, y_ref, hats_ref):
-    both = jnp.dot(two_pieces(coarse.T), y_ref[...], preferred_element_type=F32)
-    return jnp.dot(hats_ref[...], two_pieces(both[:128] + both[128:]), preferred_element_type=F32)
-
-
-def plane_sweeps(f_ref, u_ref, x_ref, q_ref, count):
+def refine(coarse, y_ref, hats_ref, p_ref, out_ref):
+    both = two_pieces(coarse.T)
+    for n in range(3):
+        part = slice(256 * n, 256 * n + 256)
+        fine = jnp.dot(both, y_ref[:, part], preferred_element_type=F32)
+        p_ref[:, part] = two_pieces(fine[:128] + fine[128:])
+    for n in range(3):
+        part = slice(256 * n, 256 * n + 256)
+        out_ref[:, part] = jnp.dot(hats_ref[...], p_ref[:, part], preferred_element_type=F32)
+
+
+def plane_sweeps(f_ref, u_ref, x_ref, q_ref, b_ref, count):
     def along_x(v, carry):
         part = pl.ds(pl.multiple_of(128 * v, 128), 128)
         for p in range(count):
-            x_ref[p, :, part] = sweep_ring(f_ref[p, :, part], u_ref[32 * p : 32 * p + 32, part], 0)[:24]
+            u = u_ref[32 * p : 32 * p + 32, part]
+            terms = remesh_terms(u, roll(u, 1, 0), roll(u, -1, 0), f_ref[p, :, part])
+            for n, m in enumerate((1, -1, 2, -2, 3, -3)):
+                if m > 0:
+                    b_ref[p, n, 0:8, :] = terms[m][24:32]
+                    b_ref[p, n, 8:32, :] = terms[m][0:24]
+                else:
+                    b_ref[p, n, 8:40, :] = terms[m]
+            total = terms[0][:24]
+            for n, m in enumerate((1, -1, 2, -2, 3, -3)):
+                total = total + b_ref[p, n, 8 - m : 32 - m, :]
+            x_ref[p, :, part] = total
         return carry
 
     lax.fori_loop(0, 6, along_x, 0)
@@ -226,11 +239,11 @@
     lax.fori_loop(0, 3, along_y, 0)
 
 
-def near_planes(s_ref, y_ref, hats_ref, hats_z_ref, outer_ref, q_ref, f_ref, c_ref, h_ref, u_ref, w_ref, x_ref):
+def near_planes(s_ref, y_ref, hats_ref, hats_z_ref, outer_ref, q_ref, f_ref, c_ref, h_ref, p_ref, u_ref, w_ref, x_ref, b_ref):
     unpack(s_ref, f_ref, c_ref, h_ref, (0, 1, 2))
-    u_ref[...] = refine(c_ref[0], y_ref, hats_ref)
-    w_ref[...] = refine(c_ref[1], y_ref, hats_z_ref)
-    plane_sweeps(f_ref, u_ref, x_ref, q_ref, 3)
+    refine(c_ref[0], y_ref, hats_ref, p_ref, u_ref)
+    refine(c_ref[1], y_ref, hats_z_ref, p_ref, w_ref)
+    plane_sweeps(f_ref, u_ref, x_ref, q_ref, b_ref, 3)
 
     def along_z(v, carry):
         part = pl.ds(pl.multiple_of(128 * v, 128), 128)
@@ -246,11 +259,11 @@
     lax.fori_loop(0, 6, along_z, 0)
 
 
-def far_plane(s_ref, y_ref, hats_ref, hats_z_ref, near_ref, own_ref, inner_ref, f_ref, c_ref, h_ref, u_ref, w_ref, x_ref, q_ref):
+def far_plane(s_ref, y_ref, hats_ref, hats_z_ref, near_ref, own_ref, inner_ref, f_ref, c_ref, h_ref, p_ref, u_ref, w_ref, x_ref, b_ref, q_ref):
     unpack(s_ref, f_ref, c_ref, h_ref, (3,))
-    u_ref[...] = refine(c_ref[0], y_ref, hats_ref)
-    w_ref[...] = refine(c_ref[1], y_ref, hats_z_ref)
-    plane_sweeps(f_ref, u_ref, x_ref, q_ref, 1)
+    refine(c_ref[0], y_ref, hats_ref, p_ref, u_ref)
+    refine(c_ref[1], y_ref, hats_z_ref, p_ref, w_ref)
+    plane_sweeps(f_ref, u_ref, x_ref, q_ref, b_ref, 1)
 
     def along_z(v, carry):
         part = pl.ds(pl.multiple_of(128 * v, 128), 128)
@@ -274,10 +287,11 @@
 
 def join(own_ref, outer_ref, inner_ref, out_ref):
     flip = odd_device() * 3
-    out_ref[0 ^ flip] = own_ref[0] + outer_ref[0]
-    out_ref[1 ^ flip] = own_ref[1] + outer_ref[1] + inner_ref[2]
-    out_ref[2 ^ flip] = own_ref[2] + outer_ref[2] + inner_ref[1]
-    out_ref[3 ^ flip] = own_ref[3] + inner_ref[0]
+    scale = 1.0 / 27.0
+    out_ref[0 ^ flip] = (own_ref[0] + outer_ref[0]) * scale
+    out_ref[1 ^ flip] = (own_ref[1] + outer_ref[1] + inner_ref[2]) * scale
+    out_ref[2 ^ flip] = (own_ref[2] + outer_ref[2] + inner_ref[1]) * scale
+    out_ref[3 ^ flip] = (own_ref[3] + inner_ref[0]) * scale
 
 
 def kernel(body, *shapes, scratch=(), flops=1e7, specs=None):
@@ -286,7 +300,7 @@
     return pl.pallas_call(
         body,
         out_shape=outs if len(outs) > 1 else outs[0],
-        scratch_shapes=[pltpu.VMEM(s, F32) for s in scratch],
+        scratch_shapes=[pltpu.VMEM(*(s if isinstance(s[0], tuple) else (s, F32))) for s in scratch],
         cost_estimate=pl.CostEstimate(flops=int(flops), transcendentals=0, bytes_accessed=1 << 20),
         compiler_params=pltpu.CompilerParams(vmem_limit_bytes=16 * 1024 * 1024),
         **extra,
@@ -298,7 +312,7 @@
 
 
 def sweep_scratch(count, speeds):
-    return [(count, 32, 768), (2, 256, 128), (32, 8, 128), (56 * count, 768), (24 * speeds, 768), (count, 24, 768)]
+    return [(count, 32, 768), (2, 256, 128), (32, 8, 128), ((256, 768), BF16), (56 * count, 768), (24 * speeds, 768), (count, 24, 768), (count, 6, 40, 128)]
 
 
 def steps(scalar, velocity):

time: 77.7 us -> 77.5 us (level)
  no operation moved by 1% of the time
where the time goes in v7:
time: 77.5 us; the launch traced here: 77.3 us
  blocking collectives  47.1 us (61%)
  waiting for transfers between devices  15.5 us (20%)
  Pallas kernels  7.59 us (10%)
  starting transfers between devices  6.49 us (8%)
    all_to_all x2, blocking collectives, exchange(): return lax.all_to_all(x, axis, split_axis=0, concat_axis=0, tiled=False)  47.1 us
    ppermute x1, waiting for transfers between devices, steps(): outer = lax.ppermute(outer, 'gz', pairs + [(b, a) for a, b in pairs])  15.5 us
    ppermute x1, starting transfers between devices, steps(): inner = lax.ppermute(inner, 'gz', pairs + [(b, a) for a, b in pairs])  3.83 us
    pallas_call x1, Pallas kernels, steps(): kernel(near_planes, (3, 24, 768), (3, 24, 768), scratch=sweep_scratch(3, 5))  2.74 us
    ppermute x1, starting transfers between devices, steps(): outer = lax.ppermute(outer, 'gz', pairs + [(b, a) for a, b in pairs])  2.66 us
    pallas_call x1, Pallas kernels, steps(): kernel(far_plane, (4, 24, 768), (3, 24, 768), scratch=sweep_scratch(1, 6)...  2.29 us
  transfers between devices with their start and end apart: 2, of which 1 were waited for; matrix products, arithmetic and copies ran while one was open for 0% of the time, Pallas kernels for 0%

profile of v7, /device:TPU:17, one launch (start us, length us, event | category | flops | bytes accessed | tf_op | source)
XLA Modules:
  0.0 77.3 jit_solution(16205311023084359310)
XLA Ops:
  0.0 0.0 copy-start.1
  0.0 0.3 shard_map.28
  0.3 0.6 copy-done.1
  0.9 0.0 copy-start
  0.9 0.5 shard_map.29
  1.4 18.3 %all_to_all.10.r_ref = f32[16,16,128]{2,1,0:T(8,128)S(1)} all-to-all(f32[16,16,128]{2,1,0:T(8,128)S(1)} %shard_map.29), channel_id=1, replica_groups=mesh['gy'=32,'gz'=16] {'gz'}, dimensions={0} | all-to-all | bytes 262144 | tf_op jit(solution)/shard_map/all_to_all | solution.py:311
  19.7 0.0 copy-done
  19.7 1.0 %shard_map.30 = f32[32,32,128]{2,1,0:T(8,128)S(1)} custom-call(f32[4,24,768]{2,1,0:T(8,128)S(1)} %copy-done, f32[16,16,128]{2,1,0:T(8,128)S(1)} %all_to_all.10.r_ref), custom_call_target="tpu_custom_call" | custom-call | flops 10000000 | bytes 1048576 | tf_op jit(solution)/shard_map/pallas_call | solution.py:323
  20.7 28.8 %all_to_all.11.s_ref = f32[32,32,128]{2,1,0:T(8,128)S(1)} all-to-all(f32[32,32,128]{2,1,0:T(8,128)S(1)} %shard_map.30), channel_id=1, replica_groups=mesh['gy'=32,'gz'=16] {'gy'}, dimensions={0} | all-to-all | bytes 1048576 | tf_op jit(solution)/shard_map/all_to_all | solution.py:311
  49.5 2.7 %shard_map.31 = (f32[3,24,768]{2,1,0:T(8,128)S(1)}, f32[3,24,768]{2,1,0:T(8,128)S(1)}) custom-call(f32[32,32,128]{2,1,0:T(8,128)S(1)} %all_to_all.11.s_ref, bf16[256,768]{1,0:T(8,128)(2,1)S(1)} %get-tuple-element.15.y_ref, bf16[168,256]{1,0:T(8,128)(2,1)S(1)} %get-tuple-element.14.after_ref.hats_ref, bf16[120,256]{1,0:T(8,128)(2,1)S(1)} %get-tuple-element.18.hats_z_ref), custom_call_target="tpu_custom_call" | custom-call | flops 10000000 | bytes 1048576 | tf_op jit(solution)/shard_map/pallas_call | solution.py:324
  52.2 2.3 %shard_map.32 = (f32[4,24,768]{2,1,0:T(8,128)S(1)}, f32[3,24,768]{2,1,0:T(8,128)S(1)}) custom-call(f32[32,32,128]{2,1,0:T(8,128)S(1)} %all_to_all.11.s_ref, bf16[256,768]{1,0:T(8,128)(2,1)S(1)} %get-tuple-element.15.y_ref, bf16[56,256]{1,0:T(8,128)(2,1)S(1)} %get-tuple-element.16.hats_ref, bf16[144,256]{1,0:T(8,128)(2,1)S(1)} %get-tuple-element.17.hats_z_ref, ...), custom_call_target="tpu_custom_call" | custom-call | flops 1000000000 | bytes 1048576 | tf_op jit(solution)/shard_map/pallas_call | solution.py:328
  54.5 3.8 %collective-permute-start.1 = (f32[3,24,768]{2,1,0:T(8,128)S(1)}, f32[3,24,768]{2,1,0:T(8,128)S(1)}, u32[]{:S(2)}, u32[]{:S(2)}) collective-permute-start(f32[3,24,768]{2,1,0:T(8,128)S(1)} %get-tuple-element.22), channel_id=1, source_target_pairs={{0,1},{2,3},{4,5},{6,7},{8,9},{10,11},{12,13},{14,15},{1,0},{3,2},... | collective-permute-start | bytes 663560 | tf_op jit(solution)/shard_map/ppermute | solution.py:330
  58.4 2.7 %collective-permute-start = (f32[3,24,768]{2,1,0:T(8,128)S(1)}, f32[3,24,768]{2,1,0:T(8,128)S(1)}, u32[]{:S(2)}, u32[]{:S(2)}) collective-permute-start(f32[3,24,768]{2,1,0:T(8,128)S(1)} %get-tuple-element.21), channel_id=1, source_target_pairs={{1,2},{3,4},{5,6},{7,8},{9,10},{11,12},{13,14},{2,1},{4,3},{6,5},{... | collective-permute-start | bytes 663560 | tf_op jit(solution)/shard_map/ppermute | solution.py:327
  61.0 0.0 collective-permute-done.1.inner_ref
  61.1 15.5 %collective-permute-done.outer_ref = f32[3,24,768]{2,1,0:T(8,128)S(1)} collective-permute-done((f32[3,24,768]{2,1,0:T(8,128)S(1)}, f32[3,24,768]{2,1,0:T(8,128)S(1)}, u32[]{:S(2)}, u32[]{:S(2)}) %collective-permute-start) | collective-permute-done | bytes 221216 | tf_op jit(solution)/shard_map/ppermute | solution.py:327
  76.5 0.8 shard_map.33
Async XLA Ops:
  0.0 0.9 %copy-start.1 = (f32[3,64,8,16]{1,3,2,0:T(8,128)S(1)}, f32[3,64,8,16]{1,3,2,0:T(8,128)}, u32[]{:S(2)}) copy-start(f32[3,64,8,16]{1,3,2,0:T(8,128)} %param.3) | copy-start | bytes 294916
  0.9 18.7 %copy-start = (f32[4,24,768]{2,1,0:T(8,128)S(1)}, f32[4,24,768]{2,1,0:T(8,128)}, u32[]{:S(2)}) copy-start(f32[4,24,768]{2,1,0:T(8,128)} %s_ref.1) | copy-start | bytes 884740
  54.5 6.5 %collective-permute-start.1 = (f32[3,24,768]{2,1,0:T(8,128)S(1)}, f32[3,24,768]{2,1,0:T(8,128)S(1)}, u32[]{:S(2)}, u32[]{:S(2)}) collective-permute-start(f32[3,24,768]{2,1,0:T(8,128)S(1)} %get-tuple-element.22), channel_id=1, source_target_pairs={{0,1},{2,3},{4,5},{6,7},{8,9},{10,11},{12,13},{14,15},{1,0},{3,2},... | collective-permute-start | bytes 663560 | tf_op jit(solution)/shard_map/ppermute | solution.py:330
  58.4 18.1 %collective-permute-start = (f32[3,24,768]{2,1,0:T(8,128)S(1)}, f32[3,24,768]{2,1,0:T(8,128)S(1)}, u32[]{:S(2)}, u32[]{:S(2)}) collective-permute-start(f32[3,24,768]{2,1,0:T(8,128)S(1)} %get-tuple-element.21), channel_id=1, source_target_pairs={{1,2},{3,4},{5,6},{7,8},{9,10},{11,12},{13,14},{2,1},{4,3},{6,5},{... | collective-permute-start | bytes 663560 | tf_op jit(solution)/shard_map/ppermute | solution.py:327

commit v8 on v7

--- a/solution.py
+++ b/solution.py
@@ -101,6 +101,7 @@
         t_ref[part, :] = block.T
     shape = (16, 8, 128)
     lane = iota(shape, 2)
+    row = iota(shape, 1)
     col = lane & 15
     slot = lane >> 4
 
@@ -120,9 +121,12 @@
         tile = jnp.where((slot < 2) & (col >= 11), roll(depth, -53, 2), tile)
         tile = jnp.where(((slot >> 1) == 1) & (col >= 11), roll(depth, -26, 2), tile)
         rest = jnp.where((slot < 4) & ((col == 7) | (col == 8)), depth, 0.0)
+        for bit in (1, 2, 4):
+            rest = jnp.where((row & bit) == 0, roll(rest, -bit, 1), roll(rest, bit, 1))
+        rest = jnp.stack([pltpu.roll(rest[n], 0, 1, stride=2, stride_axis=0) for n in range(16)])
         for bit in (4, 2, 1):
-            rest = rest + roll(roll(rest, -bit, 1), -2 * bit, 2)
-        stash.append(roll(roll(rest, 3, 1), 16, 2))
+            rest = rest + roll(rest, bit, 1)
+        stash.append(rest)
         for n in range(16):
             out_ref[2 * n + parity, 24:32, :] = tile[n]
     lane = iota((8, 128), 1)
@@ -184,7 +188,7 @@
     packed = s_ref[:, 24:32, :]
     c_ref[0] = packed.reshape(256, 128) * (1.0 / 18.0)
     rest = jnp.broadcast_to(halo[:, 3:4, :], shape).reshape(256, 128)
-    rest = jnp.stack([pltpu.roll(rest[8 * i : 8 * i + 8], 112, 1, stride=2, stride_axis=0) for i in range(32)])
+    rest = jnp.stack([pltpu.roll(rest[8 * i : 8 * i + 8], 114, 1, stride=2, stride_axis=0) for i in range(32)])
     depth = jnp.where(slot >= 4, jnp.where(col < 5, roll(packed, 53, 2), roll(packed, 26, 2)), jnp.where(col < 7, roll(packed, -73, 2), rest))
     c_ref[1] = depth.reshape(256, 128) * (1.0 / 18.0)
     for i in range(32):

time: 77.5 us -> 77.1 us (level)
  no operation moved by 1% of the time
where the time goes in v8:
time: 77.1 us; the launch traced here: 76.9 us
  blocking collectives  47.1 us (61%)
  waiting for transfers between devices  15.5 us (20%)
  Pallas kernels  7.19 us (9%)
  starting transfers between devices  6.49 us (8%)
    all_to_all x2, blocking collectives, exchange(): return lax.all_to_all(x, axis, split_axis=0, concat_axis=0, tiled=False)  47.1 us
    ppermute x1, waiting for transfers between devices, steps(): outer = lax.ppermute(outer, 'gz', pairs + [(b, a) for a, b in pairs])  15.5 us
    ppermute x1, starting transfers between devices, steps(): inner = lax.ppermute(inner, 'gz', pairs + [(b, a) for a, b in pairs])  3.83 us
    pallas_call x1, Pallas kernels, steps(): kernel(near_planes, (3, 24, 768), (3, 24, 768), scratch=sweep_scratch(3, 5))  2.74 us
    ppermute x1, starting transfers between devices, steps(): outer = lax.ppermute(outer, 'gz', pairs + [(b, a) for a, b in pairs])  2.67 us
    pallas_call x1, Pallas kernels, steps(): kernel(far_plane, (4, 24, 768), (3, 24, 768), scratch=sweep_scratch(1, 6)...  2.29 us
  transfers between devices with their start and end apart: 2, of which 1 were waited for; matrix products, arithmetic and copies ran while one was open for 0% of the time, Pallas kernels for 0%

profile of v8, /device:TPU:17, one launch (start us, length us, event | category | flops | bytes accessed | tf_op | source)
XLA Modules:
  0.0 76.9 jit_solution(5963467767545375588)
XLA Ops:
  0.0 0.0 copy-start.1
  0.0 0.3 shard_map.28
  0.3 0.6 copy-done.1
  0.9 0.0 copy-start
  0.9 0.5 shard_map.29
  1.4 18.3 %all_to_all.10.r_ref = f32[16,16,128]{2,1,0:T(8,128)S(1)} all-to-all(f32[16,16,128]{2,1,0:T(8,128)S(1)} %shard_map.29), channel_id=1, replica_groups=mesh['gy'=32,'gz'=16] {'gz'}, dimensions={0} | all-to-all | bytes 262144 | tf_op jit(solution)/shard_map/all_to_all | solution.py:315
  19.7 0.0 copy-done
  19.7 0.6 shard_map.30
  20.3 28.8 %all_to_all.11.s_ref = f32[32,32,128]{2,1,0:T(8,128)S(1)} all-to-all(f32[32,32,128]{2,1,0:T(8,128)S(1)} %shard_map.30), channel_id=1, replica_groups=mesh['gy'=32,'gz'=16] {'gy'}, dimensions={0} | all-to-all | bytes 1048576 | tf_op jit(solution)/shard_map/all_to_all | solution.py:315
  49.1 2.7 %shard_map.31 = (f32[3,24,768]{2,1,0:T(8,128)S(1)}, f32[3,24,768]{2,1,0:T(8,128)S(1)}) custom-call(f32[32,32,128]{2,1,0:T(8,128)S(1)} %all_to_all.11.s_ref, bf16[256,768]{1,0:T(8,128)(2,1)S(1)} %get-tuple-element.15.y_ref, bf16[168,256]{1,0:T(8,128)(2,1)S(1)} %get-tuple-element.14.after_ref.hats_ref, bf16[120,256]{1,0:T(8,128)(2,1)S(1)} %get-tuple-element.18.hats_z_ref), custom_call_target="tpu_custom_call" | custom-call | flops 10000000 | bytes 1048576 | tf_op jit(solution)/shard_map/pallas_call | solution.py:328
  51.8 2.3 %shard_map.32 = (f32[4,24,768]{2,1,0:T(8,128)S(1)}, f32[3,24,768]{2,1,0:T(8,128)S(1)}) custom-call(f32[32,32,128]{2,1,0:T(8,128)S(1)} %all_to_all.11.s_ref, bf16[256,768]{1,0:T(8,128)(2,1)S(1)} %get-tuple-element.15.y_ref, bf16[56,256]{1,0:T(8,128)(2,1)S(1)} %get-tuple-element.16.hats_ref, bf16[144,256]{1,0:T(8,128)(2,1)S(1)} %get-tuple-element.17.hats_z_ref, ...), custom_call_target="tpu_custom_call" | custom-call | flops 1000000000 | bytes 1048576 | tf_op jit(solution)/shard_map/pallas_call | solution.py:332
  54.1 3.8 %collective-permute-start.1 = (f32[3,24,768]{2,1,0:T(8,128)S(1)}, f32[3,24,768]{2,1,0:T(8,128)S(1)}, u32[]{:S(2)}, u32[]{:S(2)}) collective-permute-start(f32[3,24,768]{2,1,0:T(8,128)S(1)} %get-tuple-element.22), channel_id=1, source_target_pairs={{0,1},{2,3},{4,5},{6,7},{8,9},{10,11},{12,13},{14,15},{1,0},{3,2},... | collective-permute-start | bytes 663560 | tf_op jit(solution)/shard_map/ppermute | solution.py:334
  58.0 2.7 %collective-permute-start = (f32[3,24,768]{2,1,0:T(8,128)S(1)}, f32[3,24,768]{2,1,0:T(8,128)S(1)}, u32[]{:S(2)}, u32[]{:S(2)}) collective-permute-start(f32[3,24,768]{2,1,0:T(8,128)S(1)} %get-tuple-element.21), channel_id=1, source_target_pairs={{1,2},{3,4},{5,6},{7,8},{9,10},{11,12},{13,14},{2,1},{4,3},{6,5},{... | collective-permute-start | bytes 663560 | tf_op jit(solution)/shard_map/ppermute | solution.py:331
  60.6 0.0 collective-permute-done.1.inner_ref
  60.7 15.5 %collective-permute-done.outer_ref = f32[3,24,768]{2,1,0:T(8,128)S(1)} collective-permute-done((f32[3,24,768]{2,1,0:T(8,128)S(1)}, f32[3,24,768]{2,1,0:T(8,128)S(1)}, u32[]{:S(2)}, u32[]{:S(2)}) %collective-permute-start) | collective-permute-done | bytes 221216 | tf_op jit(solution)/shard_map/ppermute | solution.py:331
  76.1 0.8 shard_map.33
Async XLA Ops:
  0.0 0.9 %copy-start.1 = (f32[3,64,8,16]{1,3,2,0:T(8,128)S(1)}, f32[3,64,8,16]{1,3,2,0:T(8,128)}, u32[]{:S(2)}) copy-start(f32[3,64,8,16]{1,3,2,0:T(8,128)} %param.3) | copy-start | bytes 294916
  0.9 18.7 %copy-start = (f32[4,24,768]{2,1,0:T(8,128)S(1)}, f32[4,24,768]{2,1,0:T(8,128)}, u32[]{:S(2)}) copy-start(f32[4,24,768]{2,1,0:T(8,128)} %s_ref.1) | copy-start | bytes 884740
  54.1 6.5 %collective-permute-start.1 = (f32[3,24,768]{2,1,0:T(8,128)S(1)}, f32[3,24,768]{2,1,0:T(8,128)S(1)}, u32[]{:S(2)}, u32[]{:S(2)}) collective-permute-start(f32[3,24,768]{2,1,0:T(8,128)S(1)} %get-tuple-element.22), channel_id=1, source_target_pairs={{0,1},{2,3},{4,5},{6,7},{8,9},{10,11},{12,13},{14,15},{1,0},{3,2},... | collective-permute-start | bytes 663560 | tf_op jit(solution)/shard_map/ppermute | solution.py:334
  58.0 18.1 %collective-permute-start = (f32[3,24,768]{2,1,0:T(8,128)S(1)}, f32[3,24,768]{2,1,0:T(8,128)S(1)}, u32[]{:S(2)}, u32[]{:S(2)}) collective-permute-start(f32[3,24,768]{2,1,0:T(8,128)S(1)} %get-tuple-element.21), channel_id=1, source_target_pairs={{1,2},{3,4},{5,6},{7,8},{9,10},{11,12},{13,14},{2,1},{4,3},{6,5},{... | collective-permute-start | bytes 663560 | tf_op jit(solution)/shard_map/ppermute | solution.py:331

commit v9 on v8

--- a/solution.py
+++ b/solution.py
@@ -94,11 +94,6 @@
 
 
 def pack_chunks(s_ref, r_ref, out_ref, t_ref):
-    flip = odd_device() * 3
-    for v in range(6):
-        part = slice(128 * v, 128 * v + 128)
-        block = jnp.concatenate([s_ref[p ^ flip, :, part] for p in range(4)] + [jnp.zeros((32, 128), F32)], axis=0)
-        t_ref[part, :] = block.T
     shape = (16, 8, 128)
     lane = iota(shape, 2)
     row = iota(shape, 1)
@@ -129,6 +124,11 @@
         stash.append(rest)
         for n in range(16):
             out_ref[2 * n + parity, 24:32, :] = tile[n]
+    flip = odd_device() * 3
+    for v in range(6):
+        part = slice(128 * v, 128 * v + 128)
+        block = jnp.concatenate([s_ref[p ^ flip, :, part] for p in range(4)] + [jnp.zeros((32, 128), F32)], axis=0)
+        t_ref[part, :] = block.T
     lane = iota((8, 128), 1)
     row = iota((8, 128), 0)
     for i in range(32):
@@ -231,7 +231,7 @@
             x_ref[p, :, part] = total
         return carry
 
-    lax.fori_loop(0, 6, along_x, 0)
+    lax.fori_loop(0, 6, along_x, 0, unroll=True)
 
     def along_y(t, carry):
         for p in range(count):
@@ -260,7 +260,7 @@
             outer_ref[2, rows, part] = first[-3]
         return carry
 
-    lax.fori_loop(0, 6, along_z, 0)
+    lax.fori_loop(0, 6, along_z, 0, unroll=True)
 
 
 def far_plane(s_ref, y_ref, hats_ref, hats_z_ref, near_ref, own_ref, inner_ref, f_ref, c_ref, h_ref, p_ref, u_ref, w_ref, x_ref, b_ref, q_ref):
@@ -286,7 +286,7 @@
                 inner_ref[n, rows, part] = total[4 + n]
         return carry
 
-    lax.fori_loop(0, 6, along_z, 0)
+    lax.fori_loop(0, 6, along_z, 0, unroll=True)
 
 
 def join(own_ref, outer_ref, inner_ref, out_ref):

time: 77.1 us -> 76.4 us (level)
  no operation moved by 1% of the time
where the time goes in v9:
time: 76.4 us; the launch traced here: 76.2 us
  blocking collectives  47.1 us (62%)
  waiting for transfers between devices  15.5 us (20%)
  Pallas kernels  6.51 us (9%)
  starting transfers between devices  6.5 us (9%)
    all_to_all x2, blocking collectives, exchange(): return lax.all_to_all(x, axis, split_axis=0, concat_axis=0, tiled=False)  47.1 us
    ppermute x1, waiting for transfers between devices, steps(): outer = lax.ppermute(outer, 'gz', pairs + [(b, a) for a, b in pairs])  15.5 us
    ppermute x1, starting transfers between devices, steps(): inner = lax.ppermute(inner, 'gz', pairs + [(b, a) for a, b in pairs])  3.83 us
    ppermute x1, starting transfers between devices, steps(): outer = lax.ppermute(outer, 'gz', pairs + [(b, a) for a, b in pairs])  2.67 us
    pallas_call x1, Pallas kernels, steps(): kernel(near_planes, (3, 24, 768), (3, 24, 768), scratch=sweep_scratch(3, 5))  2.3 us
    pallas_call x1, Pallas kernels, steps(): kernel(far_plane, (4, 24, 768), (3, 24, 768), scratch=sweep_scratch(1, 6)...  2.04 us
  transfers between devices with their start and end apart: 2, of which 1 were waited for; matrix products, arithmetic and copies ran while one was open for 0% of the time, Pallas kernels for 0%

profile of v9, /device:TPU:17, one launch (start us, length us, event | category | flops | bytes accessed | tf_op | source)
XLA Modules:
  0.0 76.2 jit_solution(3871205683338573312)
XLA Ops:
  0.0 0.0 copy-start.1
  0.0 0.3 shard_map.28
  0.3 0.6 copy-done.1
  0.9 0.0 copy-start
  0.9 0.5 shard_map.29
  1.4 18.3 %all_to_all.10.r_ref = f32[16,16,128]{2,1,0:T(8,128)S(1)} all-to-all(f32[16,16,128]{2,1,0:T(8,128)S(1)} %shard_map.29), channel_id=1, replica_groups=mesh['gy'=32,'gz'=16] {'gz'}, dimensions={0} | all-to-all | bytes 262144 | tf_op jit(solution)/shard_map/all_to_all | solution.py:315
  19.7 0.0 copy-done
  19.7 0.6 shard_map.30
  20.3 28.8 %all_to_all.11.s_ref = f32[32,32,128]{2,1,0:T(8,128)S(1)} all-to-all(f32[32,32,128]{2,1,0:T(8,128)S(1)} %shard_map.30), channel_id=1, replica_groups=mesh['gy'=32,'gz'=16] {'gy'}, dimensions={0} | all-to-all | bytes 1048576 | tf_op jit(solution)/shard_map/all_to_all | solution.py:315
  49.1 2.3 %shard_map.31 = (f32[3,24,768]{2,1,0:T(8,128)S(1)}, f32[3,24,768]{2,1,0:T(8,128)S(1)}) custom-call(f32[32,32,128]{2,1,0:T(8,128)S(1)} %all_to_all.11.s_ref, bf16[256,768]{1,0:T(8,128)(2,1)S(1)} %get-tuple-element.15.y_ref, bf16[168,256]{1,0:T(8,128)(2,1)S(1)} %get-tuple-element.14.after_ref.hats_ref, bf16[120,256]{1,0:T(8,128)(2,1)S(1)} %get-tuple-element.18.hats_z_ref), custom_call_target="tpu_custom_call" | custom-call | flops 10000000 | bytes 1048576 | tf_op jit(solution)/shard_map/pallas_call | solution.py:328
  51.4 2.0 %shard_map.32 = (f32[4,24,768]{2,1,0:T(8,128)S(1)}, f32[3,24,768]{2,1,0:T(8,128)S(1)}) custom-call(f32[32,32,128]{2,1,0:T(8,128)S(1)} %all_to_all.11.s_ref, bf16[256,768]{1,0:T(8,128)(2,1)S(1)} %get-tuple-element.15.y_ref, bf16[56,256]{1,0:T(8,128)(2,1)S(1)} %get-tuple-element.16.hats_ref, bf16[144,256]{1,0:T(8,128)(2,1)S(1)} %get-tuple-element.17.hats_z_ref, ...), custom_call_target="tpu_custom_call" | custom-call | flops 1000000000 | bytes 1048576 | tf_op jit(solution)/shard_map/pallas_call | solution.py:332
  53.5 3.8 %collective-permute-start.1 = (f32[3,24,768]{2,1,0:T(8,128)S(1)}, f32[3,24,768]{2,1,0:T(8,128)S(1)}, u32[]{:S(2)}, u32[]{:S(2)}) collective-permute-start(f32[3,24,768]{2,1,0:T(8,128)S(1)} %get-tuple-element.22), channel_id=1, source_target_pairs={{0,1},{2,3},{4,5},{6,7},{8,9},{10,11},{12,13},{14,15},{1,0},{3,2},... | collective-permute-start | bytes 663560 | tf_op jit(solution)/shard_map/ppermute | solution.py:334
  57.3 2.7 %collective-permute-start = (f32[3,24,768]{2,1,0:T(8,128)S(1)}, f32[3,24,768]{2,1,0:T(8,128)S(1)}, u32[]{:S(2)}, u32[]{:S(2)}) collective-permute-start(f32[3,24,768]{2,1,0:T(8,128)S(1)} %get-tuple-element.21), channel_id=1, source_target_pairs={{1,2},{3,4},{5,6},{7,8},{9,10},{11,12},{13,14},{2,1},{4,3},{6,5},{... | collective-permute-start | bytes 663560 | tf_op jit(solution)/shard_map/ppermute | solution.py:331
  60.0 0.0 collective-permute-done.1.inner_ref
  60.0 15.5 %collective-permute-done.outer_ref = f32[3,24,768]{2,1,0:T(8,128)S(1)} collective-permute-done((f32[3,24,768]{2,1,0:T(8,128)S(1)}, f32[3,24,768]{2,1,0:T(8,128)S(1)}, u32[]{:S(2)}, u32[]{:S(2)}) %collective-permute-start) | collective-permute-done | bytes 221216 | tf_op jit(solution)/shard_map/ppermute | solution.py:331
  75.4 0.8 shard_map.33
Async XLA Ops:
  0.0 0.9 %copy-start.1 = (f32[3,64,8,16]{1,3,2,0:T(8,128)S(1)}, f32[3,64,8,16]{1,3,2,0:T(8,128)}, u32[]{:S(2)}) copy-start(f32[3,64,8,16]{1,3,2,0:T(8,128)} %param.3) | copy-start | bytes 294916
  0.9 18.7 %copy-start = (f32[4,24,768]{2,1,0:T(8,128)S(1)}, f32[4,24,768]{2,1,0:T(8,128)}, u32[]{:S(2)}) copy-start(f32[4,24,768]{2,1,0:T(8,128)} %s_ref.1) | copy-start | bytes 884740
  53.5 6.5 %collective-permute-start.1 = (f32[3,24,768]{2,1,0:T(8,128)S(1)}, f32[3,24,768]{2,1,0:T(8,128)S(1)}, u32[]{:S(2)}, u32[]{:S(2)}) collective-permute-start(f32[3,24,768]{2,1,0:T(8,128)S(1)} %get-tuple-element.22), channel_id=1, source_target_pairs={{0,1},{2,3},{4,5},{6,7},{8,9},{10,11},{12,13},{14,15},{1,0},{3,2},... | collective-permute-start | bytes 663560 | tf_op jit(solution)/shard_map/ppermute | solution.py:334
  57.3 18.1 %collective-permute-start = (f32[3,24,768]{2,1,0:T(8,128)S(1)}, f32[3,24,768]{2,1,0:T(8,128)S(1)}, u32[]{:S(2)}, u32[]{:S(2)}) collective-permute-start(f32[3,24,768]{2,1,0:T(8,128)S(1)} %get-tuple-element.21), channel_id=1, source_target_pairs={{1,2},{3,4},{5,6},{7,8},{9,10},{11,12},{13,14},{2,1},{4,3},{6,5},{... | collective-permute-start | bytes 663560 | tf_op jit(solution)/shard_map/ppermute | solution.py:331

commit v10 on v8

--- a/solution.py
+++ b/solution.py
@@ -72,7 +72,7 @@
     lane = iota((8, 128), 1)
     tiles = []
     for c in range(3):
-        block = v_ref[c].reshape(128, 64)
+        block = v_ref[c].reshape(128, 64) * (1.0 / 18.0)
         block = jnp.concatenate([block, jnp.zeros((128, 64), F32)], axis=1).T
         tiles.append([swap_blocks(block[8 * n : 8 * n + 8]) for n in range(8)])
     zero = jnp.zeros((8, 128), F32)
@@ -186,11 +186,11 @@
     halo = jnp.where(lane < 32, parts[0], jnp.where(lane < 64, parts[1], parts[2]))
     h_ref[...] = halo
     packed = s_ref[:, 24:32, :]
-    c_ref[0] = packed.reshape(256, 128) * (1.0 / 18.0)
+    c_ref[0] = packed.reshape(256, 128)
     rest = jnp.broadcast_to(halo[:, 3:4, :], shape).reshape(256, 128)
     rest = jnp.stack([pltpu.roll(rest[8 * i : 8 * i + 8], 114, 1, stride=2, stride_axis=0) for i in range(32)])
     depth = jnp.where(slot >= 4, jnp.where(col < 5, roll(packed, 53, 2), roll(packed, 26, 2)), jnp.where(col < 7, roll(packed, -73, 2), rest))
-    c_ref[1] = depth.reshape(256, 128) * (1.0 / 18.0)
+    c_ref[1] = depth.reshape(256, 128)
     for i in range(32):
         whole = jnp.concatenate([s_ref[i, 0:24, :], h_ref[i]], axis=0)
         v, at = divmod(24 * i, 128)
@@ -231,7 +231,7 @@
             x_ref[p, :, part] = total
         return carry
 
-    lax.fori_loop(0, 6, along_x, 0)
+    lax.fori_loop(0, 6, along_x, 0, unroll=True)
 
     def along_y(t, carry):
         for p in range(count):
@@ -260,7 +260,7 @@
             outer_ref[2, rows, part] = first[-3]
         return carry
 
-    lax.fori_loop(0, 6, along_z, 0)
+    lax.fori_loop(0, 6, along_z, 0, unroll=True)
 
 
 def far_plane(s_ref, y_ref, hats_ref, hats_z_ref, near_ref, own_ref, inner_ref, f_ref, c_ref, h_ref, p_ref, u_ref, w_ref, x_ref, b_ref, q_ref):
@@ -286,7 +286,7 @@
                 inner_ref[n, rows, part] = total[4 + n]
         return carry
 
-    lax.fori_loop(0, 6, along_z, 0)
+    lax.fori_loop(0, 6, along_z, 0, unroll=True)
 
 
 def join(own_ref, outer_ref, inner_ref, out_ref):

time: 77.1 us -> 76.4 us (level)
  no operation moved by 1% of the time
where the time goes in v10:
time: 76.4 us; the launch traced here: 76.2 us
  blocking collectives  47.1 us (62%)
  waiting for transfers between devices  15.5 us (20%)
  starting transfers between devices  6.51 us (9%)
  Pallas kernels  6.48 us (8%)
    all_to_all x2, blocking collectives, exchange(): return lax.all_to_all(x, axis, split_axis=0, concat_axis=0, tiled=False)  47.1 us
    ppermute x1, waiting for transfers between devices, steps(): outer = lax.ppermute(outer, 'gz', pairs + [(b, a) for a, b in pairs])  15.5 us
    ppermute x1, starting transfers between devices, steps(): inner = lax.ppermute(inner, 'gz', pairs + [(b, a) for a, b in pairs])  3.84 us
    ppermute x1, starting transfers between devices, steps(): outer = lax.ppermute(outer, 'gz', pairs + [(b, a) for a, b in pairs])  2.67 us
    pallas_call x1, Pallas kernels, steps(): kernel(near_planes, (3, 24, 768), (3, 24, 768), scratch=sweep_scratch(3, 5))  2.29 us
    pallas_call x1, Pallas kernels, steps(): kernel(far_plane, (4, 24, 768), (3, 24, 768), scratch=sweep_scratch(1, 6)...  2.03 us
  transfers between devices with their start and end apart: 2, of which 1 were waited for; matrix products, arithmetic and copies ran while one was open for 0% of the time, Pallas kernels for 0%

profile of v10, /device:TPU:17, one launch (start us, length us, event | category | flops | bytes accessed | tf_op | source)
XLA Modules:
  0.0 76.2 jit_solution(16230638228350433377)
XLA Ops:
  0.0 0.0 copy-start.1
  0.0 0.3 shard_map.28
  0.3 0.6 copy-done.1
  0.9 0.0 copy-start
  0.9 0.5 shard_map.29
  1.4 18.3 %all_to_all.10.r_ref = f32[16,16,128]{2,1,0:T(8,128)S(1)} all-to-all(f32[16,16,128]{2,1,0:T(8,128)S(1)} %shard_map.29), channel_id=1, replica_groups=mesh['gy'=32,'gz'=16] {'gz'}, dimensions={0} | all-to-all | bytes 262144 | tf_op jit(solution)/shard_map/all_to_all | solution.py:315
  19.7 0.0 copy-done
  19.7 0.6 shard_map.30
  20.3 28.8 %all_to_all.11.s_ref = f32[32,32,128]{2,1,0:T(8,128)S(1)} all-to-all(f32[32,32,128]{2,1,0:T(8,128)S(1)} %shard_map.30), channel_id=1, replica_groups=mesh['gy'=32,'gz'=16] {'gy'}, dimensions={0} | all-to-all | bytes 1048576 | tf_op jit(solution)/shard_map/all_to_all | solution.py:315
  49.1 2.3 %shard_map.31 = (f32[3,24,768]{2,1,0:T(8,128)S(1)}, f32[3,24,768]{2,1,0:T(8,128)S(1)}) custom-call(f32[32,32,128]{2,1,0:T(8,128)S(1)} %all_to_all.11.s_ref, bf16[256,768]{1,0:T(8,128)(2,1)S(1)} %get-tuple-element.15.y_ref, bf16[168,256]{1,0:T(8,128)(2,1)S(1)} %get-tuple-element.14.after_ref.hats_ref, bf16[120,256]{1,0:T(8,128)(2,1)S(1)} %get-tuple-element.18.hats_z_ref), custom_call_target="tpu_custom_call" | custom-call | flops 10000000 | bytes 1048576 | tf_op jit(solution)/shard_map/pallas_call | solution.py:328
  51.4 2.0 %shard_map.32 = (f32[4,24,768]{2,1,0:T(8,128)S(1)}, f32[3,24,768]{2,1,0:T(8,128)S(1)}) custom-call(f32[32,32,128]{2,1,0:T(8,128)S(1)} %all_to_all.11.s_ref, bf16[256,768]{1,0:T(8,128)(2,1)S(1)} %get-tuple-element.15.y_ref, bf16[56,256]{1,0:T(8,128)(2,1)S(1)} %get-tuple-element.16.hats_ref, bf16[144,256]{1,0:T(8,128)(2,1)S(1)} %get-tuple-element.17.hats_z_ref, ...), custom_call_target="tpu_custom_call" | custom-call | flops 1000000000 | bytes 1048576 | tf_op jit(solution)/shard_map/pallas_call | solution.py:332
  53.4 3.8 %collective-permute-start.1 = (f32[3,24,768]{2,1,0:T(8,128)S(1)}, f32[3,24,768]{2,1,0:T(8,128)S(1)}, u32[]{:S(2)}, u32[]{:S(2)}) collective-permute-start(f32[3,24,768]{2,1,0:T(8,128)S(1)} %get-tuple-element.22), channel_id=1, source_target_pairs={{0,1},{2,3},{4,5},{6,7},{8,9},{10,11},{12,13},{14,15},{1,0},{3,2},... | collective-permute-start | bytes 663560 | tf_op jit(solution)/shard_map/ppermute | solution.py:334
  57.3 2.7 %collective-permute-start = (f32[3,24,768]{2,1,0:T(8,128)S(1)}, f32[3,24,768]{2,1,0:T(8,128)S(1)}, u32[]{:S(2)}, u32[]{:S(2)}) collective-permute-start(f32[3,24,768]{2,1,0:T(8,128)S(1)} %get-tuple-element.21), channel_id=1, source_target_pairs={{1,2},{3,4},{5,6},{7,8},{9,10},{11,12},{13,14},{2,1},{4,3},{6,5},{... | collective-permute-start | bytes 663560 | tf_op jit(solution)/shard_map/ppermute | solution.py:331
  59.9 0.0 collective-permute-done.1.inner_ref
  60.0 15.5 %collective-permute-done.outer_ref = f32[3,24,768]{2,1,0:T(8,128)S(1)} collective-permute-done((f32[3,24,768]{2,1,0:T(8,128)S(1)}, f32[3,24,768]{2,1,0:T(8,128)S(1)}, u32[]{:S(2)}, u32[]{:S(2)}) %collective-permute-start) | collective-permute-done | bytes 221216 | tf_op jit(solution)/shard_map/ppermute | solution.py:331
  75.4 0.8 shard_map.33
Async XLA Ops:
  0.0 0.9 %copy-start.1 = (f32[3,64,8,16]{1,3,2,0:T(8,128)S(1)}, f32[3,64,8,16]{1,3,2,0:T(8,128)}, u32[]{:S(2)}) copy-start(f32[3,64,8,16]{1,3,2,0:T(8,128)} %param.3) | copy-start | bytes 294916
  0.9 18.7 %copy-start = (f32[4,24,768]{2,1,0:T(8,128)S(1)}, f32[4,24,768]{2,1,0:T(8,128)}, u32[]{:S(2)}) copy-start(f32[4,24,768]{2,1,0:T(8,128)} %s_ref.1) | copy-start | bytes 884740
  53.4 6.5 %collective-permute-start.1 = (f32[3,24,768]{2,1,0:T(8,128)S(1)}, f32[3,24,768]{2,1,0:T(8,128)S(1)}, u32[]{:S(2)}, u32[]{:S(2)}) collective-permute-start(f32[3,24,768]{2,1,0:T(8,128)S(1)} %get-tuple-element.22), channel_id=1, source_target_pairs={{0,1},{2,3},{4,5},{6,7},{8,9},{10,11},{12,13},{14,15},{1,0},{3,2},... | collective-permute-start | bytes 663560 | tf_op jit(solution)/shard_map/ppermute | solution.py:334
  57.3 18.1 %collective-permute-start = (f32[3,24,768]{2,1,0:T(8,128)S(1)}, f32[3,24,768]{2,1,0:T(8,128)S(1)}, u32[]{:S(2)}, u32[]{:S(2)}) collective-permute-start(f32[3,24,768]{2,1,0:T(8,128)S(1)} %get-tuple-element.21), channel_id=1, source_target_pairs={{1,2},{3,4},{5,6},{7,8},{9,10},{11,12},{13,14},{2,1},{4,3},{6,5},{... | collective-permute-start | bytes 663560 | tf_op jit(solution)/shard_map/ppermute | solution.py:331
